TPU v7x, 512 devices: a whole 4x8x8 slice. The times are simulated.
512 devices in a mesh: seq: 32 (over y_lo, z), head: 16 (over y_hi, x, core).
Axes of the slice: x: 4, y: 8 (y_hi: 2, y_lo: 4; y = y_hi * 4 + y_lo), z: 8, core: 2. Of those that a mesh axis runs over, the one named last changes fastest.
Arguments:
- tokens: bfloat16 [4096, 2560], P('seq'), may hold values from -51 to 51
- raw_keys: bfloat16 [131072, 768], P(('seq', 'head')), may hold values from -6 to 6
- raw_values: bfloat16 [131072, 512], P(('seq', 'head')), may hold values from -6 to 6
- query_weight: bfloat16 [2560, 12288], P('seq', 'head'), may hold values from -0.125 to 0.125
- output_weight: bfloat16 [8192, 2560], P('head', 'seq'), may hold values from -0.125 to 0.125
- key_expand: bfloat16 [192, 768], replicated, may hold values from -0.4375 to 0.4375
- key_mix: float32 [32, 768], replicated, may hold values from -1 to 1
- key_reduce: bfloat16 [768, 192], replicated, may hold values from -1.6953125 to 1.6953125
- value_expand: bfloat16 [128, 768], replicated, may hold values from -0.5 to 0.5
- value_mix: float32 [32, 768], replicated, may hold values from -1 to 1
- value_reduce: bfloat16 [768, 128], replicated, may hold values from -0.65625 to 0.65625
Outputs:
- branch_output: bfloat16 [4096, 2560], P('seq', 'head')
All inputs are finite; a program needn't handle non-finite values.
Results may differ from a plain program's by a relative error of at most 0.008.
The roundings to bfloat16 on the way count: a program that leaves them out, or rounds other values in their place, can miss the bound.
Values may be sent and summed in bfloat16 or wider, within the bound.
A program may use at most 64 MiB of HBM per device.

v0:
```python
import jax
import jax.numpy as jnp
from jax import lax
from jax.sharding import Mesh
from jax.sharding import PartitionSpec as P

G = 4
BLK = 32
STRIDE = 16
CTX_DEV = 3968
SEQ = ("seq_0", "seq_1")
SEQ_HEAD = ("seq_0", "seq_1", "head")


def shifted(block, axis, distance):
    devices = range(lax.axis_size(axis))
    route = [(i - distance, i) for i in devices if i - distance in devices]
    return lax.ppermute(block, axis, route)


def joined_along(tiles, dim):
    tiles = jnp.moveaxis(tiles, 0, dim)
    dims = tiles.shape
    return tiles.reshape(*dims[:dim], dims[dim] * dims[dim + 1], *dims[dim + 2 :])


def gather_in_order(value, axes, order):
    tiles = value
    for k in order:
        tiles = lax.all_gather(tiles, axes[k])
    done = order[::-1]
    back = [done.index(k) for k in range(len(axes))]
    tiles = tiles.transpose(*back, *range(len(axes), tiles.ndim))
    return tiles.reshape(-1, *value.shape)


def gather_axes(value, axes, order, dim):
    return joined_along(gather_in_order(value, axes, order), dim)


def from_everyone(value, axis):
    copies = jnp.broadcast_to(value, (lax.axis_size(axis), *value.shape))
    return lax.all_to_all(copies, axis, split_axis=0, concat_axis=0, tiled=True)


def gathered_copies(value, axis, dim):
    tiles = from_everyone(value, axis)
    return joined_along(tiles, dim)


def in_blocks(value, dim, peers):
    dims = value.shape
    tiles = value.reshape(*dims[:dim], peers, dims[dim] // peers, *dims[dim + 1 :])
    return jnp.moveaxis(tiles, dim, 0)


def summed_on_arrival(value, axis, dim):
    peers = lax.axis_size(axis)
    tiles = lax.all_to_all(in_blocks(value, dim, peers), axis, 0, 0, tiled=True)
    return jnp.sum(tiles, axis=0)


def project(raw, expand, groups):
    width_in = expand.shape[0]
    shaped = raw.reshape(raw.shape[0], groups, width_in)
    return jnp.einsum("tgc,ch->tgh", shaped, expand, preferred_element_type=jnp.float32)


def half_sums(projected, mix_half):
    shaped = projected.reshape(-1, STRIDE, projected.shape[1], projected.shape[2])
    return jnp.sum(shaped * mix_half[None, :, None, :], axis=1)


def finish(hidden, reduce_weight):
    activated = jax.nn.gelu(hidden, approximate=False).astype(jnp.bfloat16)
    return jnp.einsum(
        "bgh,hc->gcb", activated, reduce_weight, preferred_element_type=jnp.float32
    ).astype(jnp.bfloat16)


def attend_blocks(query_block, packed_keys, packed_values, block_ids, positions, key_span):
    key_width = packed_keys.shape[0]
    value_width = packed_values.shape[0]
    step_count = packed_keys.shape[1] // key_span
    score_scale = key_width ** (-0.5)
    rows_here = query_block.shape[0]

    def add_block(step_index, running):
        old_max, row_total, weighted = running
        key_block = lax.dynamic_slice_in_dim(packed_keys, step_index * key_span, key_span, 1)
        ids_block = lax.dynamic_slice_in_dim(block_ids, step_index * key_span, key_span, 0)
        value_block = lax.dynamic_slice_in_dim(packed_values, step_index * key_span, key_span, 1)
        scores = jnp.dot(query_block, key_block, preferred_element_type=jnp.float32) * score_scale
        visible = (STRIDE * ids_block + BLK - 1)[None, :] <= positions[:, None]
        scores = jnp.where(visible, scores, -jnp.inf)
        new_max = jnp.maximum(old_max, jnp.max(scores, axis=1))
        safe_max = jnp.where(jnp.isfinite(new_max), new_max, 0.0)
        rescale = jnp.exp(old_max - safe_max)
        exponent = jnp.exp(scores - safe_max[:, None])
        product = lax.dot_general(
            exponent.astype(jnp.bfloat16),
            value_block,
            (((1,), (1,)), ((), ())),
            preferred_element_type=jnp.float32,
        )
        return (
            new_max,
            row_total * rescale + jnp.sum(exponent, axis=1),
            weighted * rescale[:, None] + product,
        )

    start_state = (
        jnp.full((rows_here,), -jnp.inf, jnp.float32),
        jnp.zeros((rows_here,), jnp.float32),
        jnp.zeros((rows_here, value_width), jnp.float32),
    )
    return lax.fori_loop(0, step_count, add_block, start_state)


def shards(
    tokens,
    raw_keys,
    raw_values,
    query_weight,
    output_weight,
    key_expand,
    key_mix,
    key_reduce,
    value_expand,
    value_mix,
    value_reduce,
):
    groups = G
    head_count = lax.axis_size("head")
    seq_count = lax.axis_size(SEQ)
    key_width = key_expand.shape[0]
    value_width = value_expand.shape[0]
    local_tokens = raw_keys.shape[0]
    local_blocks = local_tokens // STRIDE
    row_count = tokens.shape[0]
    key_proj = project(raw_keys, key_expand, groups)
    value_proj = project(raw_values, value_expand, groups)
    tail_keys = jnp.sum(key_proj[:STRIDE] * key_mix[STRIDE:][:, None, :], axis=0)
    tail_values = jnp.sum(value_proj[:STRIDE] * value_mix[STRIDE:][:, None, :], axis=0)
    edge_keys, edge_values = shifted((tail_keys, tail_values), SEQ_HEAD, -1)
    later_keys = jnp.concatenate(
        [half_sums(key_proj[STRIDE:], key_mix[STRIDE:]), edge_keys[None]], axis=0
    )
    later_values = jnp.concatenate(
        [half_sums(value_proj[STRIDE:], value_mix[STRIDE:]), edge_values[None]], axis=0
    )
    hidden_keys = half_sums(key_proj, key_mix[:STRIDE]) + later_keys
    hidden_values = half_sums(value_proj, value_mix[:STRIDE]) + later_values
    stacked = jnp.concatenate(
        [finish(hidden_keys, key_reduce), finish(hidden_values, value_reduce)], axis=1
    )
    copies = head_count // groups
    queries = jnp.dot(
        tokens, gather_axes(query_weight, SEQ, (0, 1), 0), preferred_element_type=jnp.float32
    ).astype(jnp.bfloat16)
    heads_local = query_weight.shape[1] // key_width
    positions = (
        CTX_DEV * seq_count
        + lax.axis_index(SEQ) * row_count
        + jnp.arange(4 * row_count, dtype=jnp.int32) % row_count
    )
    slots = jnp.repeat(stacked, copies, axis=0)
    own_group = lax.all_to_all(slots, "head", split_axis=0, concat_axis=2, tiled=True)[0]
    compressed = gather_axes(own_group, SEQ, (0, 1), 1)
    block_ids = jnp.arange(compressed.shape[1], dtype=jnp.int32)
    head_sets = heads_local // 4
    query_sets = (
        queries.reshape(row_count, heads_local, key_width)
        .transpose(1, 0, 2)
        .reshape(head_sets, 4 * row_count, key_width)
    )
    packed_keys = compressed[:key_width]
    packed_values = compressed[key_width:]

    def attend(query_block):
        final_max, row_total, weighted = attend_blocks(
            query_block,
            packed_keys,
            packed_values,
            block_ids,
            positions,
            local_blocks * head_count * 8,
        )
        return (weighted / row_total[:, None]).astype(jnp.bfloat16)

    attended = lax.map(attend, query_sets).reshape(heads_local, row_count, value_width)
    attended = attended.transpose(1, 0, 2).reshape(row_count, heads_local * value_width)
    partial_out = jnp.dot(
        attended, gathered_copies(output_weight, SEQ, 1), preferred_element_type=jnp.float32
    )
    return summed_on_arrival(partial_out, "head", 1).astype(jnp.bfloat16)


def solution(mesh):
    split = Mesh(mesh.devices.reshape(4, 8, mesh.shape["head"]), ("seq_0", "seq_1", "head"))
    in_specs = (
        P(SEQ, None),
        P(SEQ_HEAD, None),
        P(SEQ_HEAD, None),
        P(SEQ, "head"),
        P("head", SEQ),
        P(),
        P(),
        P(),
        P(),
        P(),
        P(),
    )
    out_specs = P(SEQ, "head")
    return jax.shard_map(
        shards, mesh=split, in_specs=in_specs, out_specs=out_specs, check_vma=False
    )
```

profile of v0, /device:TPU:1, one launch (start us, length us, event | category | flops | bytes accessed | tf_op | source)
XLA Modules:
  0.0 302.1 jit_solution(13536420221470661202)
XLA Ops:
  6.5 15.4 %all-gather.1 = bf16[320,768]{1,0:T(8,128)(2,1)} all-gather(bf16[80,768]{1,0:T(8,128)(2,1)} %param.16), channel_id=3, replica_groups=mesh['seq_0'=4,'seq_1'=8,'head'=16] {'seq_0'}, dimensions={0}, use_global_device_ids=true | all-gather | bytes 614400 | tf_op jit(solution)/shard_map/all_gather | solution.py:30
  22.0 1.2 copy.43
  23.2 0.8 fusion.116
  24.1 1.7 multiply_reduce_fusion.1
  25.9 9.1 %collective-permute-start = (f32[4,768]{1,0:T(4,128)S(1)}, f32[4,768]{1,0:T(4,128)S(1)}, u32[]{:S(2)}, u32[]{:S(2)}) collective-permute-start(f32[4,768]{1,0:T(4,128)S(1)} %fusion.34), channel_id=1, source_target_pairs={{1,0},{2,1},{3,2},{4,3},{5,4},{6,5},{7,6},{8,7},{9,8},{10,9},{11,1... | collective-permute-start | bytes 36872 | tf_op jit(solution)/shard_map/ppermute | solution.py:18
  35.0 0.7 multiply_reduce_fusion
  35.7 1.9 collective-permute-start.1
  37.7 0.3 slice.50
  37.9 0.3 slice.52
  38.2 0.6 multiply_reduce_fusion.3
  38.8 0.6 multiply_reduce_fusion.2
  39.5 1.2 collective-permute-done.1
  40.8 0.6 fusion.20
  41.4 0.6 fusion.19
  42.1 21.8 %all_to_all.28 = bf16[16,320,16]{1,2,0:T(8,128)(2,1)S(1)} all-to-all(bf16[16,320,16]{1,2,0:T(8,128)(2,1)S(1)} %bitcast.95), channel_id=1, replica_groups=mesh['seq_0'=4,'seq_1'=8,'head'=16] {'head'}, dimensions={0} | all-to-all | bytes 327680 | tf_op jit(solution)/shard_map/all_to_all | solution.py:168
  64.0 16.9 %all_gather.21 = bf16[4,320,256]{2,1,0:T(8,128)(2,1)} all-gather(bf16[1,320,256]{2,1,0:T(8,128)(2,1)S(1)} %copy.45), channel_id=1, replica_groups=mesh['seq_0'=4,'seq_1'=8,'head'=16] {'seq_0'}, dimensions={0}, use_global_device_ids=true | all-gather | bytes 819200 | tf_op jit(solution)/shard_map/all_gather | solution.py:30
  80.9 1.9 broadcast_in_dim.67
  82.8 9.6 %all-to-all-start.1 = ((bf16[32,512,80]{1,2,0:T(8,128)(2,1)}), bf16[32,512,80]{1,2,0:T(8,128)(2,1)}, u32[]{:S(2)}, u32[]{:S(2)}) async-start(bf16[32,512,80]{1,2,0:T(8,128)(2,1)} %broadcast_in_dim.67), calls=%async_computation.1 | async-start | bytes 5242880 | tf_op jit(solution)/shard_map/all_to_all | solution.py:43
  92.4 2.4 copy.48
  94.9 0.7 convolution_convert_fusion
  95.6 0.2 copy.49
  95.7 0.1 copy.55
  95.9 110.6 %all-gather.6.cloned.1.call-done = bf16[32,320,256]{2,1,0:T(8,128)(2,1)} async-done(((bf16[4,320,256]{2,1,0:T(8,128)(2,1)}), bf16[32,320,256]{2,1,0:T(8,128)(2,1)}) %all-gather.6.cloned.1.call-update) | async-done | bytes 5242896 | tf_op jit(solution)/shard_map/all_gather | solution.py:30
  206.5 2.8 copy.46
  209.4 0.2 slice_bitcast_fusion
  209.6 1.5 slice.55
  211.1 2.0 copy.59
  213.1 3.2 %copy.51 = bf16[128,32,256]{0,2,1:T(8,128)(2,1)S(1)} copy(bf16[128,32,256]{2,0,1:T(8,128)(2,1)} %slice.55) | data formatting | bytes 4194304 | tf_op jit(solution)/shard_map/slice | solution.py:178
  216.3 34.9 %while.30 = (s32[]{:T(128)}, f32[512]{0:T(512)S(1)}, f32[512]{0:T(512)S(1)}, f32[512,128]{1,0:T(8,128)S(1)}, s32[8192]{0:T(1024)S(1)}, /*index=5*/bf16[192,8192]...) while((s32[]{:T(128)}, f32[512]{0:T(512)S(1)}, ...), condition=%wide.region_9.10_spmd.clone, body=%wide.region_6.9_spmd.clone.sunk | while | flops 679686144 | bytes 31455456 | solution.py:117
  216.4 4.3 %fusion.137 = (f32[512]{0:T(512)S(1)}, f32[512,2048]{0,1:T(8,128)}) fusion(bf16[512,192]{1,0:T(8,128)(2,1)S(1)} %get-tuple-element.517, bf16[192,8192]{1,0:T(8,128)(2,1)} %get-tuple-element.516, s32[]{:T(128)S(6)} %select_n.71, s32[512]{0:T(512)S(1)} %fusion.136, s32[2048]{0:T(1024)S(1)} %multiply_add_fusion.2), kind=kOutput, calls=%fused_computation.152.clone.1 | convolution fusion | flops 406846976 | bytes 5189636 | tf_op jit(solution)/shard_map/while/body/eval_jaxpr/while/body/eval_jaxpr/dot_general | solution.py:93
  220.7 3.0 fusion.138
  223.7 0.5 copy-done.1
  224.2 0.9 fusion.140
  225.1 4.3 %fusion.137 = (f32[512]{0:T(512)S(1)}, f32[512,2048]{0,1:T(8,128)}) fusion(bf16[512,192]{1,0:T(8,128)(2,1)S(1)} %get-tuple-element.517, bf16[192,8192]{1,0:T(8,128)(2,1)} %get-tuple-element.516, s32[]{:T(128)S(6)} %select_n.71, s32[512]{0:T(512)S(1)} %fusion.136, s32[2048]{0:T(1024)S(1)} %multiply_add_fusion.2), kind=kOutput, calls=%fused_computation.152.clone.1 | convolution fusion | flops 406846976 | bytes 5189636 | tf_op jit(solution)/shard_map/while/body/eval_jaxpr/while/body/eval_jaxpr/dot_general | solution.py:93
  229.4 3.0 fusion.138
  232.4 0.5 copy-done.1
  232.9 0.9 fusion.140
  233.8 4.3 %fusion.137 = (f32[512]{0:T(512)S(1)}, f32[512,2048]{0,1:T(8,128)}) fusion(bf16[512,192]{1,0:T(8,128)(2,1)S(1)} %get-tuple-element.517, bf16[192,8192]{1,0:T(8,128)(2,1)} %get-tuple-element.516, s32[]{:T(128)S(6)} %select_n.71, s32[512]{0:T(512)S(1)} %fusion.136, s32[2048]{0:T(1024)S(1)} %multiply_add_fusion.2), kind=kOutput, calls=%fused_computation.152.clone.1 | convolution fusion | flops 406846976 | bytes 5189636 | tf_op jit(solution)/shard_map/while/body/eval_jaxpr/while/body/eval_jaxpr/dot_general | solution.py:93
  238.2 3.0 fusion.138
  241.2 0.5 copy-done.1
  241.6 0.9 fusion.140
  242.5 4.3 %fusion.137 = (f32[512]{0:T(512)S(1)}, f32[512,2048]{0,1:T(8,128)}) fusion(bf16[512,192]{1,0:T(8,128)(2,1)S(1)} %get-tuple-element.517, bf16[192,8192]{1,0:T(8,128)(2,1)} %get-tuple-element.516, s32[]{:T(128)S(6)} %select_n.71, s32[512]{0:T(512)S(1)} %fusion.136, s32[2048]{0:T(1024)S(1)} %multiply_add_fusion.2), kind=kOutput, calls=%fused_computation.152.clone.1 | convolution fusion | flops 406846976 | bytes 5189636 | tf_op jit(solution)/shard_map/while/body/eval_jaxpr/while/body/eval_jaxpr/dot_general | solution.py:93
  246.9 3.0 fusion.138
  249.9 0.5 copy-done.1
  250.3 0.9 fusion.140
  251.6 2.6 convolution_bitcast_fusion
  254.1 40.4 %all_to_all.29 = f32[16,128,160]{1,2,0:T(8,128)S(1)} all-to-all(f32[16,128,160]{1,2,0:T(8,128)S(1)} %convolution_bitcast_fusion), channel_id=1, replica_groups=mesh['seq_0'=4,'seq_1'=8,'head'=16] {'head'}, dimensions={0} | all-to-all | bytes 2621440 | tf_op jit(solution)/shard_map/all_to_all | solution.py:59
  294.6 0.7 reduce_sum.88
  (60 shorter events, 1.0 us)
Async XLA Ops:
  6.5 88.3 %copy-start = (bf16[128,2560]{1,0:T(8,128)(2,1)S(1)}, bf16[128,2560]{1,0:T(8,128)(2,1)}, u32[]{:S(2)}) copy-start(bf16[128,2560]{1,0:T(8,128)(2,1)} %param.13) | copy-start | bytes 1966084
  6.5 28.4 %copy-start.4 = (f32[32,768]{1,0:T(8,128)S(1)}, f32[32,768]{1,0:T(8,128)}, u32[]{:S(2)}) copy-start(f32[32,768]{1,0:T(8,128)} %param.22) | copy-start | bytes 294916
  6.5 85.9 %all-gather.8.cloned.1.call-start = ((), (), s32[]{:S(2)}) async-start(), calls=%async_computation.4 | async-start | bytes 4423680 | tf_op jit(solution)/shard_map/all_gather | solution.py:30
  21.9 13.1 %copy-start.2 = (bf16[256,512]{1,0:T(8,128)(2,1)S(1)}, bf16[256,512]{1,0:T(8,128)(2,1)}, u32[]{:S(2)}) copy-start(bf16[256,512]{1,0:T(8,128)(2,1)} %param.15) | copy-start | bytes 786436
  21.9 13.1 %copy-start.3 = (bf16[128,768]{1,0:T(8,128)(2,1)S(1)}, bf16[128,768]{1,0:T(8,128)(2,1)}, u32[]{:S(2)}) copy-start(bf16[128,768]{1,0:T(8,128)(2,1)} %param.21) | copy-start | bytes 589828
  21.9 184.6 %all-gather.6.cloned.1.call-start = ((), (), s32[]{:S(2)}) async-start(), calls=%async_computation.3 | async-start | bytes 5898240 | tf_op jit(solution)/shard_map/all_gather | solution.py:30
  25.9 13.6 %collective-permute-start = (f32[4,768]{1,0:T(4,128)S(1)}, f32[4,768]{1,0:T(4,128)S(1)}, u32[]{:S(2)}, u32[]{:S(2)}) collective-permute-start(f32[4,768]{1,0:T(4,128)S(1)} %fusion.34), channel_id=1, source_target_pairs={{1,0},{2,1},{3,2},{4,3},{5,4},{6,5},{7,6},{8,7},{9,8},{10,9},{11,1... | collective-permute-start | bytes 36872 | tf_op jit(solution)/shard_map/ppermute | solution.py:18
  35.7 5.0 %collective-permute-start.1 = (f32[4,768]{1,0:T(4,128)S(1)}, f32[4,768]{1,0:T(4,128)S(1)}, u32[]{:S(2)}, u32[]{:S(2)}) collective-permute-start(f32[4,768]{1,0:T(4,128)S(1)} %fusion.33), channel_id=1, source_target_pairs={{1,0},{2,1},{3,2},{4,3},{5,4},{6,5},{7,6},{8,7},{9,8},{10,9},{11,1... | collective-permute-start | bytes 36872 | tf_op jit(solution)/shard_map/ppermute | solution.py:18
  38.2 2.6 copy-start.7
  39.5 1.9 copy-start.6
  41.4 39.6 %copy-start.5 = (bf16[512,80]{0,1:T(8,128)(2,1)S(1)}, bf16[512,80]{0,1:T(8,128)(2,1)}, u32[]{:S(2)}) copy-start(bf16[512,80]{0,1:T(8,128)(2,1)} %param.17) | copy-start | bytes 245764
  82.8 168.8 %all-to-all-start.1 = ((bf16[32,512,80]{1,2,0:T(8,128)(2,1)}), bf16[32,512,80]{1,2,0:T(8,128)(2,1)}, u32[]{:S(2)}, u32[]{:S(2)}) async-start(bf16[32,512,80]{1,2,0:T(8,128)(2,1)} %broadcast_in_dim.67), calls=%async_computation.1 | async-start | bytes 5242880 | tf_op jit(solution)/shard_map/all_to_all | solution.py:43
  220.7 3.4 %copy-start.1 = (f32[512,2048]{0,1:T(8,128)S(1)}, f32[512,2048]{0,1:T(8,128)}, u32[]{:S(2)}) copy-start(f32[512,2048]{0,1:T(8,128)} %get-tuple-element.481) | copy-start | bytes 12582916 | tf_op jit(solution)/shard_map/while/body/eval_jaxpr/while
  229.4 3.4 %copy-start.1 = (f32[512,2048]{0,1:T(8,128)S(1)}, f32[512,2048]{0,1:T(8,128)}, u32[]{:S(2)}) copy-start(f32[512,2048]{0,1:T(8,128)} %get-tuple-element.481) | copy-start | bytes 12582916 | tf_op jit(solution)/shard_map/while/body/eval_jaxpr/while
  238.2 3.4 %copy-start.1 = (f32[512,2048]{0,1:T(8,128)S(1)}, f32[512,2048]{0,1:T(8,128)}, u32[]{:S(2)}) copy-start(f32[512,2048]{0,1:T(8,128)} %get-tuple-element.481) | copy-start | bytes 12582916 | tf_op jit(solution)/shard_map/while/body/eval_jaxpr/while
  246.9 3.4 %copy-start.1 = (f32[512,2048]{0,1:T(8,128)S(1)}, f32[512,2048]{0,1:T(8,128)}, u32[]{:S(2)}) copy-start(f32[512,2048]{0,1:T(8,128)} %get-tuple-element.481) | copy-start | bytes 12582916 | tf_op jit(solution)/shard_map/while/body/eval_jaxpr/while
Sparse Core Ops, SparseCore 0:
  22.1 61.7 all-gather.7
  85.9 120.6 all-gather.5
where the time goes:
time: 303 us; the launch traced here: 302 us
  waiting for transfers between devices  112 us (37%)
  blocking collectives  94.5 us (31%)
  matrix products  27.6 us (9%)
  starting transfers between devices  20.6 us (7%)
  local copies, waits for them, and re-layouts  19.2 us (6%)
  other arithmetic  14.3 us (5%)
  between operations  13.7 us (5%)
    all_gather x2, waiting for transfers between devices, gather_in_order(): tiles = lax.all_gather(tiles, axes[k])  111 us
    all_to_all x1, blocking collectives, summed_on_arrival(): tiles = lax.all_to_all(in_blocks(value, dim, peers), axis, 0, 0, tiled=True)  40.4 us
    all_gather x2, blocking collectives, gather_in_order(): tiles = lax.all_gather(tiles, axes[k])  32.3 us
    all_to_all x1, blocking collectives, shards(): lax.all_to_all(slots, 'head', split_axis=0, concat_axis=2, tiled=True)[0]  21.8 us
    dot_general x4, matrix products, add_block(): jnp.dot(query_block, key_block, preferred_element_type=jnp.float32)  17.3 us
    reduce_sum x4, other arithmetic, add_block(): jnp.sum(exponent, axis=1)  11.9 us
    ppermute x2, starting transfers between devices, shifted(): return lax.ppermute(block, axis, route)  11 us
    all_to_all x1, starting transfers between devices, from_everyone(): return lax.all_to_all(copies, axis, split_axis=0, concat_axis=0, tiled=True)  9.57 us
  transfers between devices with their start and end apart: 5, of which 2 were waited for; matrix products, arithmetic and copies ran while one was open for 19% of the time, Pallas kernels for 0%

commit v1 on v0

v1 whole, which is shorter than its diff:
```python
import functools

import jax
import jax.numpy as jnp
from jax import lax
from jax.experimental import pallas as pl
from jax.experimental.pallas import tpu as pltpu
from jax.sharding import PartitionSpec as P

G = 4
BLK = 32
STRIDE = 16
CTX = 126976
DK = 192
DV = 128
KV_WIDTH = 384
SEQ_HEAD = ("seq", "head")
MESH = pl.DeviceIdType.MESH
BF16 = jnp.bfloat16
F32 = jnp.float32
EXP2_SCALE = DK**-0.5 * 1.4426950408889634


def shifted(block, axis, distance):
    devices = range(lax.axis_size(axis))
    route = [(i - distance, i) for i in devices if i - distance in devices]
    return lax.ppermute(block, axis, route)


def project(raw, expand, groups):
    width_in = expand.shape[0]
    shaped = raw.reshape(raw.shape[0], groups, width_in)
    return jnp.einsum("tgc,ch->tgh", shaped, expand, preferred_element_type=F32)


def half_sums(projected, mix_half):
    shaped = projected.reshape(-1, STRIDE, projected.shape[1], projected.shape[2])
    return jnp.sum(shaped * mix_half[None, :, None, :], axis=1)


def finish(hidden, reduce_weight):
    activated = jax.nn.gelu(hidden, approximate=False).astype(BF16)
    return jnp.einsum(
        "bgh,hc->gbc", activated, reduce_weight, preferred_element_type=F32
    ).astype(BF16)


def compress(raw_keys, raw_values, key_expand, key_mix, key_reduce, value_expand, value_mix, value_reduce):
    key_proj = project(raw_keys, key_expand, G)
    value_proj = project(raw_values, value_expand, G)
    tail_keys = jnp.sum(key_proj[:STRIDE] * key_mix[STRIDE:][:, None, :], axis=0)
    tail_values = jnp.sum(value_proj[:STRIDE] * value_mix[STRIDE:][:, None, :], axis=0)
    edge_keys, edge_values = shifted((tail_keys, tail_values), SEQ_HEAD, -1)
    later_keys = jnp.concatenate(
        [half_sums(key_proj[STRIDE:], key_mix[STRIDE:]), edge_keys[None]], axis=0
    )
    later_values = jnp.concatenate(
        [half_sums(value_proj[STRIDE:], value_mix[STRIDE:]), edge_values[None]], axis=0
    )
    hidden_keys = half_sums(key_proj, key_mix[:STRIDE]) + later_keys
    hidden_values = half_sums(value_proj, value_mix[:STRIDE]) + later_values
    packed_keys = finish(hidden_keys, key_reduce)
    packed_values = finish(hidden_values, value_reduce)
    pad = jnp.zeros((G, packed_keys.shape[1], KV_WIDTH - DK - DV), BF16)
    return jnp.concatenate([packed_keys, pad, packed_values], axis=2)


class Place:
    def __init__(self):
        self.s = s = lax.axis_index("seq")
        self.h = h = lax.axis_index("head")
        self.y, self.z = s // 8, s % 8
        self.g, self.j = h // 4, h % 4
        self.core = h % 2
        self.x = (h // 2) % 4
        self.y_hi = h // 8
        self.parity = self.y % 2
        self.seq_pair = (self.y + 1 - 2 * self.parity) * 8 + self.z
        self.mate = h + 1 - 2 * self.core
        self.head_pair = h + 2 - 4 * ((h // 2) % 2)
        self.head_far = (h + 8) % 16
        self.right = self.y * 8 + (self.z + 1) % 8
        self.left = self.y * 8 + (self.z + 7) % 8

    def seq_at(self, y):
        return y * 8 + self.z


def remote(src, dst, send_sem, recv_sem, seq, head):
    return pltpu.make_async_remote_copy(
        src_ref=src,
        dst_ref=dst,
        send_sem=send_sem,
        recv_sem=recv_sem,
        device_id=(seq, head),
        device_id_type=MESH,
    )


class Gather:
    def __init__(self, at, buf, rows, sems):
        self.at, self.buf, self.rows = at, buf, rows
        self.ys, self.yr, self.zs, self.zr = sems
        self.started = []

    def piece(self, i, z):
        start = pl.multiple_of(self.rows * z, 16)
        return self.buf.at[i, pl.ds(start, self.rows), :]

    def pair(self, stream, z):
        start = pl.multiple_of(self.rows * z, 16)
        return self.buf.at[pl.ds(2 * stream, 2), pl.ds(start, self.rows), :]

    def y_copy(self, i, source):
        at = self.at
        target = (at.y + 4 - i) % 4
        return remote(
            source(target), self.piece(i, at.z), self.ys.at[i], self.yr.at[i], at.seq_at(target), at.h
        )

    def start_y(self, source):
        for i in (1, 2, 3):
            copy = self.y_copy(i, source)
            copy.start()
            self.started.append(copy)

    def wait_y(self, i, source):
        self.y_copy(i, source).wait_recv()

    def z_copy(self, way, stream, step, z):
        at = self.at
        block = self.pair(stream, z)
        return remote(
            block,
            block,
            self.zs.at[way, stream, step - 1],
            self.zr.at[way, stream, step - 1],
            (at.right, at.left)[way],
            at.h,
        )

    def ways(self, stream, step):
        return (0, 1) if step < 4 else (stream,)

    def send_z(self, stream, step):
        at = self.at
        for way in self.ways(stream, step):
            z = (at.z + 8 - (step - 1)) % 8 if way == 0 else (at.z + step - 1) % 8
            copy = self.z_copy(way, stream, step, z)
            copy.start()
            self.started.append(copy)

    def came_from(self, way, step):
        at = self.at
        return (at.z + 8 - step) % 8 if way == 0 else (at.z + step) % 8

    def wait_z(self, stream, step):
        for way in self.ways(stream, step):
            self.z_copy(way, stream, step, self.came_from(way, step)).wait_recv()

    def finish_sends(self):
        for copy in self.started:
            copy.wait_send()


def attend_half(who, at, qbuf, stacked, kvb, scores, lane_max, store):
    for half in range(2):
        for head in range(2):
            rows = pl.ds((2 * half + head) * 128, 128)
            stacked[rows, 0:DK] = qbuf[who, half, :, head * DK : (head + 1) * DK]
    lane_max[...] = jnp.full_like(lane_max, -jnp.inf)
    last = (3 + 4 - at.y) % 4
    first_position = CTX + at.s * 128
    half_index = (at.h // 2) % 2

    def score_chunk(chunk, carry):
        keys = kvb[chunk // 4, chunk % 4, :, 0:256]
        block = lax.dot_general(
            stacked[...], keys, (((1,), (1,)), ((), ())), preferred_element_type=F32
        )
        scores[chunk] = block

        @pl.when(chunk % 4 == last)
        def _():
            tail = scores[chunk, :, 384:512]
            column = lax.broadcasted_iota(jnp.int32, tail.shape, 1)
            row = lax.broadcasted_iota(jnp.int32, tail.shape, 0) % 128
            ids = 256 * (30 + column // 64) + 64 * (2 * half_index + chunk // 4) + column % 64
            visible = STRIDE * ids + BLK - 1 <= first_position + row
            scores[chunk, :, 384:512] = jnp.where(visible, tail, -jnp.inf)

        top = lane_max[...]
        for k in range(4):
            top = jnp.maximum(top, scores[chunk, :, 128 * k : 128 * (k + 1)])
        lane_max[...] = top
        return carry

    lax.fori_loop(0, 8, score_chunk, 0)

    for head in range(4):
        rows = slice(head * 128, (head + 1) * 128)
        row_max = jnp.max(lane_max[rows, :], axis=1, keepdims=True)

        def weigh_chunk(chunk, carry):
            total, numerator = carry
            exponent = jnp.exp2((scores[chunk, rows, :] - row_max) * EXP2_SCALE)
            for k in range(4):
                total = total + exponent[:, 128 * k : 128 * (k + 1)]
            values = kvb[chunk // 4, chunk % 4, :, 256:384]
            numerator = numerator + jnp.dot(
                exponent.astype(BF16), values, preferred_element_type=F32
            )
            return total, numerator

        start = jnp.zeros((128, 128), F32)
        total, numerator = lax.fori_loop(0, 8, weigh_chunk, (start, start))
        row_total = jnp.sum(total, axis=1, keepdims=True)
        store(head, row_max, row_total, numerator)


def kernel(
    tokens,
    kv4,
    qw,
    ow,
    out,
    qwb,
    owb,
    kvb,
    tokp,
    qbuf,
    qother,
    stacked,
    scores,
    lane_max,
    mine,
    mine_max,
    mine_total,
    part,
    stats,
    part_in,
    stats_in,
    attended,
    summed,
    o1,
    o1_in,
    o2,
    o2_in,
    o3,
    o3_in,
    q_ys, q_yr, q_zs, q_zr,
    k_ys, k_yr, k_zs, k_zr,
    o_ys, o_yr, o_zs, o_zr,
    r_s, r_r,
    m_s, m_r,
    e_s, e_r,
):
    at = Place()
    s, h, c = at.s, at.h, at.core

    barrier = pltpu.get_barrier_semaphore()
    partners = [(s, (h + d) % 16) for d in range(1, 16)]
    partners += [(at.seq_at((at.y + d) % 4), h) for d in (1, 2, 3)]
    partners += [(at.right, h), (at.left, h), (at.seq_pair, at.head_pair)]
    for partner in partners:
        pl.semaphore_signal(barrier, inc=1, device_id=partner, device_id_type=MESH)
    pl.semaphore_wait(barrier, len(partners))

    started = []

    def go(copy):
        copy.start()
        started.append(copy)
        return copy

    q = Gather(at, qwb, 80, (q_ys, q_yr, q_zs, q_zr))
    o = Gather(at, owb, 80, (o_ys, o_yr, o_zs, o_zr))
    k = Gather(at, kvb.at[c], 64, (k_ys, k_yr, k_zs, k_zr))

    own_rows = pl.ds(pl.multiple_of(64 * at.z + 16 * at.j, 16), 16)

    def spread_copy(group):
        quarter = at.g % 2
        return remote(
            kv4.at[group],
            kvb.at[quarter, 0, own_rows, :],
            r_s.at[group],
            r_r.at[at.j],
            s,
            4 * group + at.g,
        )

    for group in range(G):
        @pl.when(4 * group + at.g != h)
        def _(group=group):
            spread_copy(group).start()

        @pl.when(4 * group + at.g == h)
        def _(group=group):
            kvb[c, 0, own_rows, :] = kv4[group]

    def q_source(target):
        return qw.at[:, pl.ds(pl.multiple_of(384 * (target % 2), 128), 384)]

    q.start_y(q_source)
    qwb[0, pl.ds(pl.multiple_of(80 * at.z, 16), 80), :] = qw[
        :, pl.ds(pl.multiple_of(384 * at.parity, 128), 384)
    ]
    tok_copy = go(remote(tokens, tokp, e_s.at[0], e_r.at[0], at.seq_pair, h))
    q.wait_y(1, q_source)
    q.send_z(0, 1)
    q.wait_y(2, q_source)
    q.wait_y(3, q_source)
    q.send_z(1, 1)

    for m in range(4):
        @pl.when(4 * at.j + m != h)
        def _(m=m):
            rows = pl.ds(pl.multiple_of(64 * at.z + 16 * m, 16), 16)
            remote(
                kv4.at[0], kvb.at[c, 0, rows, :], r_s.at[0], r_r.at[m], s, 4 * at.j + m
            ).wait_recv()

    def k_source(target):
        return k.piece(0, at.z)

    k.start_y(k_source)

    def mate_copy(quarter, stream, index, z):
        start = pl.multiple_of(64 * z, 16)
        block = kvb.at[quarter, pl.ds(2 * stream, 2), pl.ds(start, 64), :]
        return remote(
            block, block, m_s.at[stream, index], m_r.at[stream, index], s, at.mate
        )

    def k_arrived(stream, step):
        k.wait_z(stream, step)
        for way in k.ways(stream, step):
            index = 7 if step == 4 else 3 * way + step
            go(mate_copy(c, stream, index, k.came_from(way, step)))

    def q_round(step):
        for stream in (0, 1):
            q.wait_z(stream, step - 1)
            q.send_z(stream, step)

    def k_round(step):
        for stream in (0, 1):
            k_arrived(stream, step - 1)
            k.send_z(stream, step)

    q_round(2)
    k.wait_y(1, k_source)
    k.send_z(0, 1)
    go(mate_copy(c, 0, 0, at.z))
    k.wait_y(2, k_source)
    k.wait_y(3, k_source)
    k.send_z(1, 1)
    go(mate_copy(c, 1, 0, at.z))
    ow_source = lambda target: ow
    o.start_y(ow_source)
    owb[0, pl.ds(pl.multiple_of(80 * at.z, 16), 80), :] = ow[...]
    q_round(3)
    k_round(2)
    q_round(4)
    k_round(3)
    q.wait_z(0, 4)
    q.wait_z(1, 4)
    tok_copy.wait_recv()

    def project_queries(source):
        total = jnp.zeros((128, 384), F32)
        for i in range(4):
            start = pl.multiple_of(640 * ((at.y + i) % 4), 128)
            total = total + jnp.dot(
                source[:, pl.ds(start, 640)], qwb[i], preferred_element_type=F32
            )
        return total.astype(BF16)

    qother[...] = project_queries(tokp)
    q_in = [
        remote(qother, qbuf.at[0, at.parity], e_s.at[1], e_r.at[1], at.seq_pair, h),
        remote(qother, qbuf.at[1, at.parity], e_s.at[2], e_r.at[2], at.seq_pair, at.head_pair),
    ]
    go(q_in[0])
    go(q_in[1])
    qbuf[0, at.parity] = project_queries(tokens)
    q_in.append(
        go(
            remote(
                qbuf.at[0, at.parity], qbuf.at[1, at.parity], e_s.at[3], e_r.at[3], s, at.head_pair
            )
        )
    )
    k_round(4)
    o.wait_y(1, ow_source)
    o.send_z(0, 1)
    o.wait_y(2, ow_source)
    o.wait_y(3, ow_source)
    o.send_z(1, 1)
    k_arrived(0, 4)
    k_arrived(1, 4)
    stacked[:, DK:] = jnp.zeros((512, 256 - DK), BF16)
    q_in[0].wait_recv()
    q_in[2].wait_recv()
    q_in[1].wait_recv()
    for stream in (0, 1):
        mate_copy(1 - c, stream, 0, at.z).wait_recv()
        for step in (1, 2, 3, 4):
            for way in k.ways(stream, step):
                index = 7 if step == 4 else 3 * way + step
                mate_copy(1 - c, stream, index, k.came_from(way, step)).wait_recv()

    lane = lax.broadcasted_iota(jnp.int32, (128, 128), 1)

    def store_part(head, row_max, row_total, numerator):
        part[head] = numerator.astype(BF16)
        tile = jnp.where(lane == 0, row_max, jnp.where(lane == 1, row_total, 0.0))
        stats[head] = jnp.transpose(tile)[0:8, :]

    attend_half(1, at, qbuf, stacked, kvb, scores, lane_max, store_part)
    part_copy = go(remote(part, part_in, e_s.at[4], e_r.at[4], s, at.head_pair))
    stat_copy = go(remote(stats, stats_in, e_s.at[5], e_r.at[5], s, at.head_pair))
    for stream in (0, 1):
        o.wait_z(stream, 1)
        o.send_z(stream, 2)

    def store_mine(head, row_max, row_total, numerator):
        mine[head] = numerator
        mine_max[head] = jnp.broadcast_to(row_max, (128, 128))
        mine_total[head] = jnp.broadcast_to(row_total, (128, 128))

    attend_half(0, at, qbuf, stacked, kvb, scores, lane_max, store_mine)
    for stream in (0, 1):
        o.wait_z(stream, 2)
        o.send_z(stream, 3)
    part_copy.wait_recv()
    stat_copy.wait_recv()
    for head in range(4):
        tile = jnp.concatenate([stats_in[head], jnp.zeros((120, 128), F32)], axis=0)
        tile = jnp.transpose(tile)
        other_max = jnp.broadcast_to(tile[:, 0:1], (128, 128))
        other_total = jnp.broadcast_to(tile[:, 1:2], (128, 128))
        top = jnp.maximum(mine_max[head], other_max)
        own_part = jnp.exp2((mine_max[head] - top) * EXP2_SCALE)
        other_part = jnp.exp2((other_max - top) * EXP2_SCALE)
        total = mine_total[head] * own_part + other_total * other_part
        value = mine[head] * own_part + part_in[head].astype(F32) * other_part
        attended[:, head * DV : (head + 1) * DV] = (value / total).astype(BF16)
    for stream in (0, 1):
        o.wait_z(stream, 3)
        o.send_z(stream, 4)
    o.wait_z(0, 4)
    o.wait_z(1, 4)

    for i in range(4):
        start = pl.multiple_of(4 * ((at.y + i) % 4), 4)
        block = lax.dot_general(
            owb[i], attended[...], (((1,), (1,)), ((), ())), preferred_element_type=F32
        ).reshape(2, 2, 160, 128)
        summed[pl.ds(2 * ((at.y + i) % 4), 2)] = block
        o1[pl.ds(2 * ((at.y + i) % 4), 2)] = block.astype(BF16)
    mate_sum = go(remote(o1.at[:, 1 - c], o1_in, e_s.at[6], e_r.at[6], s, at.mate))
    mate_sum.wait_recv()
    for i in range(8):
        summed[i, 0] = summed[i, c] + o1_in[i].astype(F32)
        o2[i // 4, i % 4] = summed[i, 0].astype(BF16)
    x_sums = []
    for d in (1, 2, 3):
        x = (at.x + d) % 4
        x_sums.append(
            go(
                remote(
                    o2.at[:, x], o2_in.at[d - 1], e_s.at[6 + d], e_r.at[6 + d], s, 8 * at.y_hi + 2 * x + c
                )
            )
        )
    for copy in x_sums:
        copy.wait_recv()
    far = 1 - at.y_hi
    value = summed[4 * far + at.x, 0]
    for d in range(3):
        value = value + o2_in[d, far].astype(F32)
    o3[...] = value.astype(BF16)
    y_sum = go(remote(o3, o3_in, e_s.at[10], e_r.at[10], s, at.head_far))
    value = summed[4 * at.y_hi + at.x, 0]
    for d in range(3):
        value = value + o2_in[d, at.y_hi].astype(F32)
    y_sum.wait_recv()
    out[...] = (value + o3_in[...].astype(F32)).astype(BF16)

    for copy in started:
        copy.wait_send()
    for gather in (q, k, o):
        gather.finish_sends()
    for group in range(G):
        @pl.when(4 * group + at.g != h)
        def _(group=group):
            spread_copy(group).wait_send()


def shards(
    tokens,
    raw_keys,
    raw_values,
    query_weight,
    output_weight,
    key_expand,
    key_mix,
    key_reduce,
    value_expand,
    value_mix,
    value_reduce,
):
    kv4 = compress(
        raw_keys, raw_values, key_expand, key_mix, key_reduce, value_expand, value_mix, value_reduce
    )
    vmem = pltpu.VMEM
    dma = pltpu.SemaphoreType.DMA
    ring = [dma((4,)), dma((4,)), dma((2, 2, 4)), dma((2, 2, 4))]
    out = pl.pallas_call(
        kernel,
        out_shape=jax.ShapeDtypeStruct((160, 128), BF16),
        in_specs=[pl.BlockSpec(memory_space=vmem)] * 4,
        out_specs=pl.BlockSpec(memory_space=vmem),
        scratch_shapes=[
            vmem((4, 640, 384), BF16),
            vmem((4, 640, 512), BF16),
            vmem((2, 4, 512, KV_WIDTH), BF16),
            vmem((128, 2560), BF16),
            vmem((2, 2, 128, 384), BF16),
            vmem((128, 384), BF16),
            vmem((512, 256), BF16),
            vmem((8, 512, 512), F32),
            vmem((512, 128), F32),
            vmem((4, 128, 128), F32),
            vmem((4, 128, 128), F32),
            vmem((4, 128, 128), F32),
            vmem((4, 128, 128), BF16),
            vmem((4, 8, 128), F32),
            vmem((4, 128, 128), BF16),
            vmem((4, 8, 128), F32),
            vmem((128, 512), BF16),
            vmem((8, 2, 160, 128), F32),
            vmem((8, 2, 160, 128), BF16),
            vmem((8, 160, 128), BF16),
            vmem((2, 4, 160, 128), BF16),
            vmem((3, 2, 160, 128), BF16),
            vmem((160, 128), BF16),
            vmem((160, 128), BF16),
            *ring,
            *ring,
            *ring,
            dma((4,)),
            dma((4,)),
            dma((2, 8)),
            dma((2, 8)),
            dma((11,)),
            dma((11,)),
        ],
        compiler_params=pltpu.CompilerParams(
            collective_id=0, has_side_effects=True, vmem_limit_bytes=56 * 1024 * 1024
        ),
        name="branch",
    )(tokens, kv4, query_weight, output_weight.T)
    return out.T


def solution(mesh):
    in_specs = (
        P("seq", None),
        P(SEQ_HEAD, None),
        P(SEQ_HEAD, None),
        P("seq", "head"),
        P("head", "seq"),
        P(),
        P(),
        P(),
        P(),
        P(),
        P(),
    )
    return jax.shard_map(
        shards, mesh=mesh, in_specs=in_specs, out_specs=P("seq", "head"), check_vma=False
    )
```

time: 303 us -> 141 us (0.47)
  Pallas kernels: 0 us -> 116 us
  waiting for transfers between devices: 112 us -> 0.01 us
  blocking collectives: 94.5 us -> 0 us
  matrix products: 27.6 us -> 5.31 us
  between operations: 13.7 us -> 0.14 us
  local copies, waits for them, and re-layouts: 19.2 us -> 6.16 us
  other arithmetic: 14.3 us -> 1.95 us
  starting transfers between devices: 20.6 us -> 10.7 us
    pallas_call x0 -> x1, Pallas kernels: none -> 116 us  [shards(): pl.pallas_call(kernel, out_shape=jax.ShapeDtypeStruct((160, 128), BF16),...]
    all_gather x2 -> x0, waiting for transfers between devices: 111 us -> none  [gather_in_order(): tiles = lax.all_gather(tiles, axes[k])]
    all_to_all x2 -> x0, blocking collectives: 62.2 us -> none  [the longest x1 40.4 us: summed_on_arrival(): tiles = lax.all_to_all(in_blocks(value, dim, peers), axis, 0, 0, tiled=True)]
    all_gather x2 -> x0, blocking collectives: 32.3 us -> none  [gather_in_order(): tiles = lax.all_gather(tiles, axes[k])]
    dot_general x14 -> x4, matrix products: 27.6 us -> 5.31 us  [the longest x2 4.14 us: project(): return jnp.einsum('tgc,ch->tgh', shaped, expand, preferred_element_type=F32)]
    reduce_sum x7 -> x2, other arithmetic: 12.7 us -> 0.09 us  [the longest x1 0.05 us: compress(): jnp.sum(key_proj[:STRIDE] * key_mix[STRIDE:][:, None, :], axis=0)]
    all_to_all x1 -> x0, starting transfers between devices: 9.57 us -> none  [from_everyone(): return lax.all_to_all(copies, axis, split_axis=0, concat_axis=0, tiled=True)]
    slice x7 -> x4, local copies, waits for them, and re-layouts: 8.1 us -> 2.02 us  [the longest x1 0.88 us: compress(): value_mix[STRIDE:]]
  transfers between devices with their start and end apart: 5 -> 2, of which waited for: 2 -> 0; matrix products, arithmetic and copies ran while one was open for 19% -> 5% of each run, Pallas kernels for 0% -> 0%
where the time goes in v1:
time: 141 us; the launch traced here: 140 us
  Pallas kernels  116 us (82%)
  starting transfers between devices  10.7 us (8%)
  local copies, waits for them, and re-layouts  6.16 us (4%)
  matrix products  5.31 us (4%)
  other arithmetic  1.95 us (1%)
    pallas_call x1, Pallas kernels, shards(): pl.pallas_call(kernel, out_shape=jax.ShapeDtypeStruct((160, 128), BF16),...  116 us
    ppermute x2, starting transfers between devices, shifted(): return lax.ppermute(block, axis, route)  10.7 us
    dot_general x2, matrix products, project(): return jnp.einsum('tgc,ch->tgh', shaped, expand, preferred_element_type=F32)  4.14 us
    unnamed x12, local copies, waits for them, and re-layouts  3.33 us
  transfers between devices with their start and end apart: 2, of which 0 were waited for; matrix products, arithmetic and copies ran while one was open for 5% of the time, Pallas kernels for 0%

profile of v1, /device:TPU:1, one launch (start us, length us, event | category | flops | bytes accessed | tf_op | source)
XLA Modules:
  0.0 140.1 jit_solution(11907702186449258065)
XLA Ops:
  0.0 0.0 copy-start
  0.0 0.0 copy-start.2
  0.0 0.9 fusion.97
  0.9 2.4 %multiply_reduce_fusion = (f32[16,4,768]{2,0,1:T(8,128)}, f32[256,4,768]{2,0,1:T(8,128)S(1)}) fusion(f32[16,768]{1,0:T(8,128)S(1)} %get-tuple-element.8, bf16[128,768]{1,0:T(8,128)(2,1)} %param.19, bf16[256,512]{1,0:T(8,128)(2,1)} %param.13), kind=kOutput, calls=%fused_computation | convolution fusion | flops 202850304 | bytes 3850240 | tf_op jit(solution)/shard_map/tgc,ch->tgh/dot_general | solution.py:33
  3.3 8.7 %collective-permute-start.1 = (f32[4,768]{1,0:T(4,128)S(1)}, f32[4,768]{1,0:T(4,128)}, u32[]{:S(2)}, u32[]{:S(2)}) collective-permute-start(f32[4,768]{1,0:T(4,128)S(1)} %fusion.14), channel_id=1, source_target_pairs={{1,0},{2,1},{3,2},{4,3},{5,4},{6,5},{7,6},{8,7},{9,8},{10,9},{11,1... | collective-permute-start | bytes 36872 | tf_op jit(solution)/shard_map/ppermute | solution.py:27
  12.1 0.0 copy-done.2
  12.1 0.6 fusion.96
  12.7 1.9 %copy.14 = bf16[256,768]{0,1:T(8,128)(2,1)} copy(bf16[256,768]{1,0:T(8,128)(2,1)} %param.12) | data formatting | bytes 786432 | tf_op args[1]
  14.6 0.0 copy-done
  14.6 1.8 %multiply_reduce_fusion.1 = (f32[16,4,768]{2,0,1:T(8,128)S(1)}, f32[256,4,768]{2,0,1:T(8,128)S(1)}) fusion(f32[16,768]{1,0:T(8,128)} %get-tuple-element.6, bf16[256,4,192]{0,2,1:T(8,128)(2,1)} %bitcast.41, bf16[192,768]{1,0:T(8,128)(2,1)S(1)} %copy-done), kind=kOutput, calls=%fused_computation.1 | convolution fusion | flops 303513600 | bytes 4079616 | tf_op jit(solution)/shard_map/tgc,ch->tgh/dot_general | solution.py:33
  16.4 1.9 %collective-permute-start = (f32[4,768]{1,0:T(4,128)S(1)}, f32[4,768]{1,0:T(4,128)S(1)}, u32[]{:S(2)}, u32[]{:S(2)}) collective-permute-start(f32[4,768]{1,0:T(4,128)S(1)} %fusion.15), channel_id=1, source_target_pairs={{1,0},{2,1},{3,2},{4,3},{5,4},{6,5},{7,6},{8,7},{9,8},{10,9},{11,1... | collective-permute-start | bytes 36872 | tf_op jit(solution)/shard_map/ppermute | solution.py:27
  18.4 0.3 slice.36
  18.6 0.3 slice.34
  18.9 0.0 copy-start.1
  18.9 0.0 copy-start.4
  18.9 0.6 multiply_reduce_fusion.2
  19.5 0.6 multiply_reduce_fusion.3
  20.1 0.0 copy-start.3
  20.2 0.1 pad.1.clone
  20.2 0.0 collective-permute-done.1
  20.3 0.7 broadcast_in_dim.8
  21.0 0.0 copy-done.1
  21.0 0.0 copy-done.4
  21.0 0.6 fusion.1
  21.6 0.0 collective-permute-done
  21.6 0.0 copy-done.3
  21.6 0.6 fusion
  22.2 0.6 pad_maximum_fusion.kv4
  22.8 115.9 %branch.1 = bf16[160,128]{1,0:T(8,128)(2,1)} custom-call(bf16[128,2560]{1,0:T(8,128)(2,1)} %tokens.1, bf16[4,16,384]{2,1,0:T(8,128)(2,1)} %pad_maximum_fusion.kv4, bf16[80,768]{1,0:T(8,128)(2,1)} %qw.1, bf16[80,512]{1,0:T(8,128)(2,1)} %bitcast.43), custom_call_target="tpu_custom_call" | custom-call | tf_op jit(solution)/shard_map/branch/pallas_call | solution.py:521
  138.7 1.4 copy.24
  (4 shorter events, 0.1 us)
Async XLA Ops:
  0.0 14.6 %copy-start = (bf16[192,768]{1,0:T(8,128)(2,1)S(1)}, bf16[192,768]{1,0:T(8,128)(2,1)}, u32[]{:S(2)}) copy-start(bf16[192,768]{1,0:T(8,128)(2,1)} %param.16) | copy-start | bytes 884740
  0.0 12.1 %copy-start.2 = (f32[32,768]{1,0:T(8,128)S(1)}, f32[32,768]{1,0:T(8,128)}, u32[]{:S(2)}) copy-start(f32[32,768]{1,0:T(8,128)} %param.17) | copy-start | bytes 294916
  3.3 17.0 %collective-permute-start.1 = (f32[4,768]{1,0:T(4,128)S(1)}, f32[4,768]{1,0:T(4,128)}, u32[]{:S(2)}, u32[]{:S(2)}) collective-permute-start(f32[4,768]{1,0:T(4,128)S(1)} %fusion.14), channel_id=1, source_target_pairs={{1,0},{2,1},{3,2},{4,3},{5,4},{6,5},{7,6},{8,7},{9,8},{10,9},{11,1... | collective-permute-start | bytes 36872 | tf_op jit(solution)/shard_map/ppermute | solution.py:27
  16.4 5.1 %collective-permute-start = (f32[4,768]{1,0:T(4,128)S(1)}, f32[4,768]{1,0:T(4,128)S(1)}, u32[]{:S(2)}, u32[]{:S(2)}) collective-permute-start(f32[4,768]{1,0:T(4,128)S(1)} %fusion.15), channel_id=1, source_target_pairs={{1,0},{2,1},{3,2},{4,3},{5,4},{6,5},{7,6},{8,7},{9,8},{10,9},{11,1... | collective-permute-start | bytes 36872 | tf_op jit(solution)/shard_map/ppermute | solution.py:27
  18.9 2.1 %copy-start.1 = (f32[16,4,768]{2,0,1:T(8,128)S(1)}, f32[16,4,768]{2,0,1:T(8,128)}, u32[]{:S(2)}) copy-start(f32[16,4,768]{2,0,1:T(8,128)} %get-tuple-element.9) | copy-start | bytes 589828
  18.9 2.1 %copy-start.4 = (bf16[768,128]{1,0:T(8,128)(2,1)S(1)}, bf16[768,128]{1,0:T(8,128)(2,1)}, u32[]{:S(2)}) copy-start(bf16[768,128]{1,0:T(8,128)(2,1)} %param.21) | copy-start | bytes 589828
  20.1 1.4 %copy-start.3 = (bf16[768,192]{0,1:T(8,128)(2,1)S(1)}, bf16[768,192]{0,1:T(8,128)(2,1)}, u32[]{:S(2)}) copy-start(bf16[768,192]{0,1:T(8,128)(2,1)} %param.18) | copy-start | bytes 884740

commit v2 on v1

--- a/solution.py
+++ b/solution.py
@@ -1,5 +1,3 @@
-import functools
-
 import jax
 import jax.numpy as jnp
 from jax import lax
@@ -21,48 +19,28 @@
 EXP2_SCALE = DK**-0.5 * 1.4426950408889634
 
 
-def shifted(block, axis, distance):
-    devices = range(lax.axis_size(axis))
-    route = [(i - distance, i) for i in devices if i - distance in devices]
-    return lax.ppermute(block, axis, route)
-
-
-def project(raw, expand, groups):
-    width_in = expand.shape[0]
-    shaped = raw.reshape(raw.shape[0], groups, width_in)
-    return jnp.einsum("tgc,ch->tgh", shaped, expand, preferred_element_type=F32)
-
-
-def half_sums(projected, mix_half):
-    shaped = projected.reshape(-1, STRIDE, projected.shape[1], projected.shape[2])
-    return jnp.sum(shaped * mix_half[None, :, None, :], axis=1)
-
-
-def finish(hidden, reduce_weight):
-    activated = jax.nn.gelu(hidden, approximate=False).astype(BF16)
-    return jnp.einsum(
-        "bgh,hc->gbc", activated, reduce_weight, preferred_element_type=F32
-    ).astype(BF16)
-
-
-def compress(raw_keys, raw_values, key_expand, key_mix, key_reduce, value_expand, value_mix, value_reduce):
-    key_proj = project(raw_keys, key_expand, G)
-    value_proj = project(raw_values, value_expand, G)
-    tail_keys = jnp.sum(key_proj[:STRIDE] * key_mix[STRIDE:][:, None, :], axis=0)
-    tail_values = jnp.sum(value_proj[:STRIDE] * value_mix[STRIDE:][:, None, :], axis=0)
-    edge_keys, edge_values = shifted((tail_keys, tail_values), SEQ_HEAD, -1)
-    later_keys = jnp.concatenate(
-        [half_sums(key_proj[STRIDE:], key_mix[STRIDE:]), edge_keys[None]], axis=0
-    )
-    later_values = jnp.concatenate(
-        [half_sums(value_proj[STRIDE:], value_mix[STRIDE:]), edge_values[None]], axis=0
-    )
-    hidden_keys = half_sums(key_proj, key_mix[:STRIDE]) + later_keys
-    hidden_values = half_sums(value_proj, value_mix[:STRIDE]) + later_values
-    packed_keys = finish(hidden_keys, key_reduce)
-    packed_values = finish(hidden_values, value_reduce)
-    pad = jnp.zeros((G, packed_keys.shape[1], KV_WIDTH - DK - DV), BF16)
-    return jnp.concatenate([packed_keys, pad, packed_values], axis=2)
+def compress_part(raw, edge, has_next, expands, starts, mix, reduce_weight, order, moved, projected, hidden):
+    moved[0:256, :] = jnp.dot(order, raw[...], preferred_element_type=F32).astype(BF16)
+    moved[256:272, :] = jnp.where(has_next, edge[...], jnp.zeros_like(edge))
+    row = lax.broadcasted_iota(jnp.int32, (16, 768), 0)
+    for group in range(G):
+        expand = expands[group]
+        start = starts[group]
+        projected[...] = jnp.dot(
+            moved[:, start : start + expand.shape[0]], expand, preferred_element_type=F32
+        )
+        first = jnp.zeros((16, 768), F32)
+        second = jnp.zeros((16, 768), F32)
+        for p in range(STRIDE):
+            block = projected[16 * p : 16 * p + 16, :]
+            first = first + block * mix[p : p + 1, :]
+            second = second + block * mix[STRIDE + p : STRIDE + p + 1, :]
+        beyond = jnp.sum(projected[256:272, :] * mix[STRIDE:, :], axis=0, keepdims=True)
+        later = jnp.where(row == 15, beyond, pltpu.roll(second, 15, 0))
+        hidden[16 * group : 16 * group + 16, :] = first + later
+    value = hidden[...]
+    activated = (0.5 * value * (1.0 + lax.erf(value * 0.5**0.5))).astype(BF16)
+    return jnp.dot(activated, reduce_weight[...], preferred_element_type=F32).astype(BF16)
 
 
 class Place:
@@ -168,62 +146,79 @@
         for head in range(2):
             rows = pl.ds((2 * half + head) * 128, 128)
             stacked[rows, 0:DK] = qbuf[who, half, :, head * DK : (head + 1) * DK]
-    lane_max[...] = jnp.full_like(lane_max, -jnp.inf)
     last = (3 + 4 - at.y) % 4
     first_position = CTX + at.s * 128
     half_index = (at.h // 2) % 2
 
-    def score_chunk(chunk, carry):
-        keys = kvb[chunk // 4, chunk % 4, :, 0:256]
+    def entry(n):
+        return n // 4, (last + n % 4) % 4
+
+    def score_chunk(n, masked):
+        quarter, i = entry(n)
         block = lax.dot_general(
-            stacked[...], keys, (((1,), (1,)), ((), ())), preferred_element_type=F32
-        )
-        scores[chunk] = block
-
-        @pl.when(chunk % 4 == last)
-        def _():
-            tail = scores[chunk, :, 384:512]
-            column = lax.broadcasted_iota(jnp.int32, tail.shape, 1)
-            row = lax.broadcasted_iota(jnp.int32, tail.shape, 0) % 128
-            ids = 256 * (30 + column // 64) + 64 * (2 * half_index + chunk // 4) + column % 64
+            stacked[...], kvb[quarter, i, :, 0:256], (((1,), (1,)), ((), ())), preferred_element_type=F32
+        )
+        parts = [block[:, 128 * k : 128 * (k + 1)] for k in range(4)]
+        if masked:
+            column = lax.broadcasted_iota(jnp.int32, (512, 128), 1)
+            row = lax.broadcasted_iota(jnp.int32, (512, 128), 0) % 128
+            ids = 256 * (30 + column // 64) + 64 * (2 * half_index + quarter) + column % 64
             visible = STRIDE * ids + BLK - 1 <= first_position + row
-            scores[chunk, :, 384:512] = jnp.where(visible, tail, -jnp.inf)
-
-        top = lane_max[...]
+            parts[3] = jnp.where(visible, parts[3], -jnp.inf)
         for k in range(4):
-            top = jnp.maximum(top, scores[chunk, :, 128 * k : 128 * (k + 1)])
-        lane_max[...] = top
+            scores[n, :, 128 * k : 128 * (k + 1)] = parts[k]
+        return jnp.maximum(jnp.maximum(parts[0], parts[1]), jnp.maximum(parts[2], parts[3]))
+
+    lane_max[...] = jnp.maximum(score_chunk(0, True), score_chunk(4, True))
+
+    def other_chunk(n, carry):
+        lane_max[...] = jnp.maximum(lane_max[...], score_chunk(n + n // 3 + 1, False))
         return carry
 
-    lax.fori_loop(0, 8, score_chunk, 0)
+    lax.fori_loop(0, 6, other_chunk, 0, unroll=6)
 
     for head in range(4):
         rows = slice(head * 128, (head + 1) * 128)
         row_max = jnp.max(lane_max[rows, :], axis=1, keepdims=True)
 
-        def weigh_chunk(chunk, carry):
+        def weigh_chunk(n, carry):
             total, numerator = carry
-            exponent = jnp.exp2((scores[chunk, rows, :] - row_max) * EXP2_SCALE)
+            exponent = jnp.exp2((scores[n, rows, :] - row_max) * EXP2_SCALE)
             for k in range(4):
                 total = total + exponent[:, 128 * k : 128 * (k + 1)]
-            values = kvb[chunk // 4, chunk % 4, :, 256:384]
+            quarter, i = entry(n)
             numerator = numerator + jnp.dot(
-                exponent.astype(BF16), values, preferred_element_type=F32
+                exponent.astype(BF16), kvb[quarter, i, :, 256:384], preferred_element_type=F32
             )
             return total, numerator
 
         start = jnp.zeros((128, 128), F32)
-        total, numerator = lax.fori_loop(0, 8, weigh_chunk, (start, start))
-        row_total = jnp.sum(total, axis=1, keepdims=True)
-        store(head, row_max, row_total, numerator)
+        total, numerator = lax.fori_loop(0, 8, weigh_chunk, (start, start), unroll=8)
+        store(head, row_max, jnp.sum(total, axis=1, keepdims=True), numerator)
 
 
 def kernel(
     tokens,
+    raw_keys,
+    raw_values,
+    qw,
+    ow_in,
+    key_expand,
+    key_mix,
+    key_reduce,
+    value_expand,
+    value_mix,
+    value_reduce,
+    out,
+    edge_keys,
+    edge_values,
+    moved_keys,
+    moved_values,
+    placed_expand,
+    projected,
+    hidden,
     kv4,
-    qw,
     ow,
-    out,
     qwb,
     owb,
     kvb,
@@ -262,6 +257,9 @@
     partners = [(s, (h + d) % 16) for d in range(1, 16)]
     partners += [(at.seq_at((at.y + d) % 4), h) for d in (1, 2, 3)]
     partners += [(at.right, h), (at.left, h), (at.seq_pair, at.head_pair)]
+    flat = 16 * s + h
+    before, after = (flat + 511) % 512, (flat + 1) % 512
+    partners += [(before // 16, before % 16), (after // 16, after % 16)]
     for partner in partners:
         pl.semaphore_signal(barrier, inc=1, device_id=partner, device_id_type=MESH)
     pl.semaphore_wait(barrier, len(partners))
@@ -276,6 +274,82 @@
     q = Gather(at, qwb, 80, (q_ys, q_yr, q_zs, q_zr))
     o = Gather(at, owb, 80, (o_ys, o_yr, o_zs, o_zr))
     k = Gather(at, kvb.at[c], 64, (k_ys, k_yr, k_zs, k_zr))
+
+    edge_in = [
+        remote(source.at[0:16], target, e_s.at[i], e_r.at[i], before // 16, before % 16)
+        for i, (source, target) in enumerate(((raw_keys, edge_keys), (raw_values, edge_values)), 11)
+    ]
+    for copy in edge_in:
+        go(copy)
+
+    def q_source(target):
+        return qw.at[:, pl.ds(pl.multiple_of(384 * (target % 2), 128), 384)]
+
+    q.start_y(q_source)
+    half_tokens = pl.ds(pl.multiple_of(1280 * c, 128), 1280)
+    tok_copy = go(
+        remote(
+            tokens.at[:, half_tokens], tokp.at[:, half_tokens], e_s.at[0], e_r.at[0], at.seq_pair, h
+        )
+    )
+    qwb[0, pl.ds(pl.multiple_of(80 * at.z, 16), 80), :] = qw[
+        :, pl.ds(pl.multiple_of(384 * at.parity, 128), 384)
+    ]
+
+    same = lax.broadcasted_iota(jnp.int32, (80, 80), 0) == lax.broadcasted_iota(jnp.int32, (80, 80), 1)
+    ow[...] = lax.dot_general(
+        same.astype(F32).astype(BF16), ow_in[...], (((1,), (1,)), ((), ())), preferred_element_type=F32
+    ).astype(BF16)
+    owb[0, pl.ds(pl.multiple_of(80 * at.z, 16), 80), :] = ow[...]
+    placed_expand[0, 0:DK, :] = key_expand[...]
+    placed_expand[0, DK:256, :] = jnp.zeros((256 - DK, 768), BF16)
+    placed_expand[1, 0 : 256 - DK, :] = jnp.zeros((256 - DK, 768), BF16)
+    placed_expand[1, 256 - DK :, :] = key_expand[...]
+    stacked[:, DK:] = jnp.zeros((512, 256 - DK), BF16)
+
+    q.wait_y(1, q_source)
+    q.send_z(0, 1)
+    q.wait_y(2, q_source)
+    q.wait_y(3, q_source)
+    q.send_z(1, 1)
+
+    row = lax.broadcasted_iota(jnp.int32, (256, 256), 0)
+    column = lax.broadcasted_iota(jnp.int32, (256, 256), 1)
+    order = (column == 16 * (row % 16) + row // 16).astype(F32).astype(BF16)
+    for copy in edge_in:
+        copy.wait_recv()
+    has_next = flat < 511
+    packed_keys = compress_part(
+        raw_keys,
+        edge_keys,
+        has_next,
+        [placed_expand[group % 2] for group in range(G)],
+        (0, 128, 384, 512),
+        key_mix,
+        key_reduce,
+        order,
+        moved_keys,
+        projected,
+        hidden,
+    )
+    packed_values = compress_part(
+        raw_values,
+        edge_values,
+        has_next,
+        [value_expand[...]] * G,
+        (0, 128, 256, 384),
+        value_mix,
+        value_reduce,
+        order,
+        moved_values,
+        projected,
+        hidden,
+    )
+    for group in range(G):
+        rows = slice(16 * group, 16 * group + 16)
+        kv4[group, :, 0:DK] = packed_keys[rows, :]
+        kv4[group, :, DK:256] = jnp.zeros((16, 256 - DK), BF16)
+        kv4[group, :, 256:384] = packed_values[rows, :]
 
     own_rows = pl.ds(pl.multiple_of(64 * at.z + 16 * at.j, 16), 16)
 
@@ -299,20 +373,36 @@
         def _(group=group):
             kvb[c, 0, own_rows, :] = kv4[group]
 
-    def q_source(target):
-        return qw.at[:, pl.ds(pl.multiple_of(384 * (target % 2), 128), 384)]
-
-    q.start_y(q_source)
-    qwb[0, pl.ds(pl.multiple_of(80 * at.z, 16), 80), :] = qw[
-        :, pl.ds(pl.multiple_of(384 * at.parity, 128), 384)
-    ]
-    tok_copy = go(remote(tokens, tokp, e_s.at[0], e_r.at[0], at.seq_pair, h))
-    q.wait_y(1, q_source)
-    q.send_z(0, 1)
-    q.wait_y(2, q_source)
-    q.wait_y(3, q_source)
-    q.send_z(1, 1)
-
+    def k_source(target):
+        return k.piece(0, at.z)
+
+    def ow_source(target):
+        return ow
+
+    def mate_copy(quarter, stream, index, z):
+        start = pl.multiple_of(64 * z, 16)
+        block = kvb.at[quarter, pl.ds(2 * stream, 2), pl.ds(start, 64), :]
+        return remote(
+            block, block, m_s.at[stream, index], m_r.at[stream, index], s, at.mate
+        )
+
+    def k_arrived(stream, step):
+        k.wait_z(stream, step)
+        for way in k.ways(stream, step):
+            index = 7 if step == 4 else 3 * way + step
+            go(mate_copy(c, stream, index, k.came_from(way, step)))
+
+    def q_round(step):
+        for stream in (0, 1):
+            q.wait_z(stream, step - 1)
+            q.send_z(stream, step)
+
+    def k_round(step):
+        for stream in (0, 1):
+            k_arrived(stream, step - 1)
+            k.send_z(stream, step)
+
+    q_round(2)
     for m in range(4):
         @pl.when(4 * at.j + m != h)
         def _(m=m):
@@ -320,36 +410,9 @@
             remote(
                 kv4.at[0], kvb.at[c, 0, rows, :], r_s.at[0], r_r.at[m], s, 4 * at.j + m
             ).wait_recv()
-
-    def k_source(target):
-        return k.piece(0, at.z)
-
     k.start_y(k_source)
-
-    def mate_copy(quarter, stream, index, z):
-        start = pl.multiple_of(64 * z, 16)
-        block = kvb.at[quarter, pl.ds(2 * stream, 2), pl.ds(start, 64), :]
-        return remote(
-            block, block, m_s.at[stream, index], m_r.at[stream, index], s, at.mate
-        )
-
-    def k_arrived(stream, step):
-        k.wait_z(stream, step)
-        for way in k.ways(stream, step):
-            index = 7 if step == 4 else 3 * way + step
-            go(mate_copy(c, stream, index, k.came_from(way, step)))
-
-    def q_round(step):
-        for stream in (0, 1):
-            q.wait_z(stream, step - 1)
-            q.send_z(stream, step)
-
-    def k_round(step):
-        for stream in (0, 1):
-            k_arrived(stream, step - 1)
-            k.send_z(stream, step)
-
-    q_round(2)
+    o.start_y(ow_source)
+    q_round(3)
     k.wait_y(1, k_source)
     k.send_z(0, 1)
     go(mate_copy(c, 0, 0, at.z))
@@ -357,16 +420,15 @@
     k.wait_y(3, k_source)
     k.send_z(1, 1)
     go(mate_copy(c, 1, 0, at.z))
-    ow_source = lambda target: ow
-    o.start_y(ow_source)
-    owb[0, pl.ds(pl.multiple_of(80 * at.z, 16), 80), :] = ow[...]
-    q_round(3)
+    tok_copy.wait_recv()
+    arrived_tokens = tokp.at[:, half_tokens]
+    go(remote(arrived_tokens, arrived_tokens, e_s.at[13], e_r.at[13], s, at.mate))
+    q_round(4)
     k_round(2)
-    q_round(4)
-    k_round(3)
+    other_half = tokp.at[:, pl.ds(pl.multiple_of(1280 - 1280 * c, 128), 1280)]
+    remote(other_half, other_half, e_s.at[13], e_r.at[13], s, at.mate).wait_recv()
     q.wait_z(0, 4)
     q.wait_z(1, 4)
-    tok_copy.wait_recv()
 
     def project_queries(source):
         total = jnp.zeros((128, 384), F32)
@@ -392,6 +454,7 @@
             )
         )
     )
+    k_round(3)
     k_round(4)
     o.wait_y(1, ow_source)
     o.send_z(0, 1)
@@ -400,7 +463,6 @@
     o.send_z(1, 1)
     k_arrived(0, 4)
     k_arrived(1, 4)
-    stacked[:, DK:] = jnp.zeros((512, 256 - DK), BF16)
     q_in[0].wait_recv()
     q_in[2].wait_recv()
     q_in[1].wait_recv()
@@ -512,18 +574,24 @@
     value_mix,
     value_reduce,
 ):
-    kv4 = compress(
-        raw_keys, raw_values, key_expand, key_mix, key_reduce, value_expand, value_mix, value_reduce
-    )
     vmem = pltpu.VMEM
     dma = pltpu.SemaphoreType.DMA
     ring = [dma((4,)), dma((4,)), dma((2, 2, 4)), dma((2, 2, 4))]
     out = pl.pallas_call(
         kernel,
         out_shape=jax.ShapeDtypeStruct((160, 128), BF16),
-        in_specs=[pl.BlockSpec(memory_space=vmem)] * 4,
+        in_specs=[pl.BlockSpec(memory_space=vmem)] * 11,
         out_specs=pl.BlockSpec(memory_space=vmem),
         scratch_shapes=[
+            vmem((16, 768), BF16),
+            vmem((16, 512), BF16),
+            vmem((272, 768), BF16),
+            vmem((272, 512), BF16),
+            vmem((2, 256, 768), BF16),
+            vmem((272, 768), F32),
+            vmem((64, 768), F32),
+            vmem((G, 16, KV_WIDTH), BF16),
+            vmem((80, 512), BF16),
             vmem((4, 640, 384), BF16),
             vmem((4, 640, 512), BF16),
             vmem((2, 4, 512, KV_WIDTH), BF16),
@@ -555,14 +623,26 @@
             dma((4,)),
             dma((2, 8)),
             dma((2, 8)),
-            dma((11,)),
-            dma((11,)),
+            dma((14,)),
+            dma((14,)),
         ],
         compiler_params=pltpu.CompilerParams(
             collective_id=0, has_side_effects=True, vmem_limit_bytes=56 * 1024 * 1024
         ),
         name="branch",
-    )(tokens, kv4, query_weight, output_weight.T)
+    )(
+        tokens,
+        raw_keys,
+        raw_values,
+        query_weight,
+        output_weight,
+        key_expand,
+        key_mix,
+        key_reduce,
+        value_expand,
+        value_mix,
+        value_reduce,
+    )
     return out.T
 
 

time: 141 us -> 111 us (0.79)
  starting transfers between devices: 10.7 us -> 0 us
  Pallas kernels: 116 us -> 106 us
  matrix products: 5.31 us -> 0 us
  other arithmetic: 1.95 us -> 0 us
    ppermute x2 -> x0, starting transfers between devices: 10.7 us -> none  [shifted(): return lax.ppermute(block, axis, route)]
    pallas_call x1, Pallas kernels: 116 us -> 106 us  [shards(): pl.pallas_call(kernel, out_shape=jax.ShapeDtypeStruct((160, 128), BF16),...]
    dot_general x4 -> x0, matrix products: 5.31 us -> none  [the longest x2 4.14 us: project(): return jnp.einsum('tgc,ch->tgh', shaped, expand, preferred_element_type=F32)]
    slice x4 -> x0, local copies, waits for them, and re-layouts: 2.02 us -> none  [the longest x1 0.88 us: compress(): value_mix[STRIDE:]]
    unnamed x12 -> x3, local copies, waits for them, and re-layouts: 3.33 us -> 4.91 us
  transfers between devices with their start and end apart: 2 -> 0, of which waited for: 0 -> 0; matrix products, arithmetic and copies ran while one was open for 5% -> 0% of each run, Pallas kernels for 0% -> 0%
where the time goes in v2:
time: 111 us
  Pallas kernels  106 us (95%)
  local copies, waits for them, and re-layouts  4.91 us (4%)
    pallas_call x1, Pallas kernels, shards(): pl.pallas_call(kernel, out_shape=jax.ShapeDtypeStruct((160, 128), BF16),...  106 us
    unnamed x3, local copies, waits for them, and re-layouts  4.91 us

profile of v2, /device:TPU:1, one launch (start us, length us, event | category | flops | bytes accessed | tf_op | source)
XLA Modules:
  0.0 110.8 jit_solution(8156291581247215249)
XLA Ops:
  0.0 1.6 %copy.12.ow_in = bf16[512,80]{1,0:T(8,128)(2,1)} copy(bf16[512,80]{0,1:T(8,128)(2,1)} %param.15) | data formatting | bytes 163840 | tf_op args[4]
  1.6 1.9 %copy.13.key_reduce = bf16[768,192]{1,0:T(8,128)(2,1)} copy(bf16[768,192]{0,1:T(8,128)(2,1)} %param.18) | data formatting | bytes 589824 | tf_op args[7]
  3.5 105.9 %branch.1 = bf16[160,128]{1,0:T(8,128)(2,1)} custom-call(bf16[128,2560]{1,0:T(8,128)(2,1)} %tokens.1, bf16[256,768]{1,0:T(8,128)(2,1)} %raw_keys.1, bf16[256,512]{1,0:T(8,128)(2,1)} %raw_values.1, bf16[80,768]{1,0:T(8,128)(2,1)} %qw.1, bf16[512,80]{1,0:T(8,128)(2,1)} %copy.12.ow_in, bf16[192,768]{1,0:T(8,128)(2,1)} %key_expand.1, f32[32,768]{1,0:T(8,128)} %key_mix.1, ...), custom_call_target="tpu_custom_call" | custom-call | tf_op jit(solution)/shard_map/branch/pallas_call | solution.py:580
  109.4 1.4 %copy.15 = bf16[128,160]{0,1:T(8,128)(2,1)} copy(bf16[128,160]{0,1:T(8,128)(2,1)} %bitcast.1) | data formatting | bytes 81920

commit v3 on v2

--- a/solution.py
+++ b/solution.py
@@ -19,7 +19,9 @@
 EXP2_SCALE = DK**-0.5 * 1.4426950408889634
 
 
-def compress_part(raw, edge, has_next, expands, starts, mix, reduce_weight, order, moved, projected, hidden):
+def compress_part(
+    raw, edge, has_next, expands, starts, mix, reduce_weight, reduce_dim, order, moved, projected, hidden
+):
     moved[0:256, :] = jnp.dot(order, raw[...], preferred_element_type=F32).astype(BF16)
     moved[256:272, :] = jnp.where(has_next, edge[...], jnp.zeros_like(edge))
     row = lax.broadcasted_iota(jnp.int32, (16, 768), 0)
@@ -40,7 +42,9 @@
         hidden[16 * group : 16 * group + 16, :] = first + later
     value = hidden[...]
     activated = (0.5 * value * (1.0 + lax.erf(value * 0.5**0.5))).astype(BF16)
-    return jnp.dot(activated, reduce_weight[...], preferred_element_type=F32).astype(BF16)
+    return lax.dot_general(
+        activated, reduce_weight[...], (((1,), (reduce_dim,)), ((), ())), preferred_element_type=F32
+    ).astype(BF16)
 
 
 class Place:
@@ -76,8 +80,8 @@
 
 
 class Gather:
-    def __init__(self, at, buf, rows, sems):
-        self.at, self.buf, self.rows = at, buf, rows
+    def __init__(self, at, buf, rows, streams, sems):
+        self.at, self.buf, self.rows, self.streams = at, buf, rows, streams
         self.ys, self.yr, self.zs, self.zr = sems
         self.started = []
 
@@ -85,9 +89,10 @@
         start = pl.multiple_of(self.rows * z, 16)
         return self.buf.at[i, pl.ds(start, self.rows), :]
 
-    def pair(self, stream, z):
+    def block(self, stream, z):
+        first, count, _ = self.streams[stream]
         start = pl.multiple_of(self.rows * z, 16)
-        return self.buf.at[pl.ds(2 * stream, 2), pl.ds(start, self.rows), :]
+        return self.buf.at[pl.ds(first, count), pl.ds(start, self.rows), :]
 
     def y_copy(self, i, source):
         at = self.at
@@ -102,12 +107,17 @@
             copy.start()
             self.started.append(copy)
 
-    def wait_y(self, i, source):
-        self.y_copy(i, source).wait_recv()
+    def first_z(self, source, streams):
+        for stream in streams:
+            first, count, _ = self.streams[stream]
+            for i in range(first, first + count):
+                if i > 0:
+                    self.y_copy(i, source).wait_recv()
+            self.send_z(stream, 1)
 
     def z_copy(self, way, stream, step, z):
         at = self.at
-        block = self.pair(stream, z)
+        block = self.block(stream, z)
         return remote(
             block,
             block,
@@ -118,7 +128,7 @@
         )
 
     def ways(self, stream, step):
-        return (0, 1) if step < 4 else (stream,)
+        return (0, 1) if step < 4 else (self.streams[stream][2],)
 
     def send_z(self, stream, step):
         at = self.at
@@ -136,9 +146,64 @@
         for way in self.ways(stream, step):
             self.z_copy(way, stream, step, self.came_from(way, step)).wait_recv()
 
+    def next_z(self, step):
+        for stream in range(len(self.streams)):
+            self.wait_z(stream, step - 1)
+            self.send_z(stream, step)
+
+    def end_z(self):
+        for stream in range(len(self.streams)):
+            self.wait_z(stream, 4)
+
     def finish_sends(self):
         for copy in self.started:
             copy.wait_send()
+
+
+class HalfGather(Gather):
+    def half_copy(self, n, source):
+        at = self.at
+        i = at.y % 2
+        target = at.y // 2 + 2 * n
+        return target, remote(
+            source, self.piece(i, at.z), self.ys.at[n], self.yr.at[i], at.seq_at(target), at.h
+        )
+
+    def start_half(self, source):
+        at = self.at
+        for n in range(2):
+            target, copy = self.half_copy(n, source)
+
+            @pl.when(target != at.y)
+            def _(copy=copy):
+                copy.start()
+
+            @pl.when(target == at.y)
+            def _():
+                start = pl.multiple_of(self.rows * at.z, 16)
+                self.buf[at.y % 2, pl.ds(start, self.rows), :] = source[...]
+
+    def wait_half(self, i, source):
+        at = self.at
+        origin = 2 * at.parity + i
+
+        @pl.when(origin != at.y)
+        def _():
+            remote(
+                source, self.piece(i, at.z), self.ys.at[i], self.yr.at[i], at.seq_at(origin), at.h
+            ).wait_recv()
+
+    def end_half(self, source):
+        for n in range(2):
+            target, copy = self.half_copy(n, source)
+
+            @pl.when(target != self.at.y)
+            def _(copy=copy):
+                copy.wait_send()
+
+
+QUARTERS = ((0, 1, 0), (1, 2, 1), (3, 1, 0))
+HALVES = ((0, 1, 0), (1, 1, 1))
 
 
 def attend_half(who, at, qbuf, stacked, kvb, scores, lane_max, store):
@@ -202,7 +267,7 @@
     raw_keys,
     raw_values,
     qw,
-    ow_in,
+    ow,
     key_expand,
     key_mix,
     key_reduce,
@@ -218,7 +283,6 @@
     projected,
     hidden,
     kv4,
-    ow,
     qwb,
     owb,
     kvb,
@@ -256,7 +320,8 @@
     barrier = pltpu.get_barrier_semaphore()
     partners = [(s, (h + d) % 16) for d in range(1, 16)]
     partners += [(at.seq_at((at.y + d) % 4), h) for d in (1, 2, 3)]
-    partners += [(at.right, h), (at.left, h), (at.seq_pair, at.head_pair)]
+    partners += [(at.right, h), (at.left, h)]
+    partners += [(at.seq_pair, at.head_pair), (at.seq_pair, at.head_far)]
     flat = 16 * s + h
     before, after = (flat + 511) % 512, (flat + 1) % 512
     partners += [(before // 16, before % 16), (after // 16, after % 16)]
@@ -271,9 +336,9 @@
         started.append(copy)
         return copy
 
-    q = Gather(at, qwb, 80, (q_ys, q_yr, q_zs, q_zr))
-    o = Gather(at, owb, 80, (o_ys, o_yr, o_zs, o_zr))
-    k = Gather(at, kvb.at[c], 64, (k_ys, k_yr, k_zs, k_zr))
+    q = Gather(at, qwb, 80, QUARTERS, (q_ys, q_yr, q_zs, q_zr))
+    o = HalfGather(at, owb, 80, HALVES, (o_ys, o_yr, o_zs, o_zr))
+    k = Gather(at, kvb.at[c], 64, QUARTERS, (k_ys, k_yr, k_zs, k_zr))
 
     edge_in = [
         remote(source.at[0:16], target, e_s.at[i], e_r.at[i], before // 16, before % 16)
@@ -285,33 +350,24 @@
     def q_source(target):
         return qw.at[:, pl.ds(pl.multiple_of(384 * (target % 2), 128), 384)]
 
+    qwb[0, pl.ds(pl.multiple_of(80 * at.z, 16), 80), :] = qw[
+        :, pl.ds(pl.multiple_of(384 * at.parity, 128), 384)
+    ]
     q.start_y(q_source)
+    q.first_z(q_source, (0,))
     half_tokens = pl.ds(pl.multiple_of(1280 * c, 128), 1280)
     tok_copy = go(
         remote(
             tokens.at[:, half_tokens], tokp.at[:, half_tokens], e_s.at[0], e_r.at[0], at.seq_pair, h
         )
     )
-    qwb[0, pl.ds(pl.multiple_of(80 * at.z, 16), 80), :] = qw[
-        :, pl.ds(pl.multiple_of(384 * at.parity, 128), 384)
-    ]
-
-    same = lax.broadcasted_iota(jnp.int32, (80, 80), 0) == lax.broadcasted_iota(jnp.int32, (80, 80), 1)
-    ow[...] = lax.dot_general(
-        same.astype(F32).astype(BF16), ow_in[...], (((1,), (1,)), ((), ())), preferred_element_type=F32
-    ).astype(BF16)
-    owb[0, pl.ds(pl.multiple_of(80 * at.z, 16), 80), :] = ow[...]
     placed_expand[0, 0:DK, :] = key_expand[...]
     placed_expand[0, DK:256, :] = jnp.zeros((256 - DK, 768), BF16)
     placed_expand[1, 0 : 256 - DK, :] = jnp.zeros((256 - DK, 768), BF16)
     placed_expand[1, 256 - DK :, :] = key_expand[...]
     stacked[:, DK:] = jnp.zeros((512, 256 - DK), BF16)
 
-    q.wait_y(1, q_source)
-    q.send_z(0, 1)
-    q.wait_y(2, q_source)
-    q.wait_y(3, q_source)
-    q.send_z(1, 1)
+    q.first_z(q_source, (1, 2))
 
     row = lax.broadcasted_iota(jnp.int32, (256, 256), 0)
     column = lax.broadcasted_iota(jnp.int32, (256, 256), 1)
@@ -327,6 +383,7 @@
         (0, 128, 384, 512),
         key_mix,
         key_reduce,
+        1,
         order,
         moved_keys,
         projected,
@@ -340,6 +397,7 @@
         (0, 128, 256, 384),
         value_mix,
         value_reduce,
+        0,
         order,
         moved_values,
         projected,
@@ -376,12 +434,10 @@
     def k_source(target):
         return k.piece(0, at.z)
 
-    def ow_source(target):
-        return ow
-
     def mate_copy(quarter, stream, index, z):
+        first, count, _ = QUARTERS[stream]
         start = pl.multiple_of(64 * z, 16)
-        block = kvb.at[quarter, pl.ds(2 * stream, 2), pl.ds(start, 64), :]
+        block = kvb.at[quarter, pl.ds(first, count), pl.ds(start, 64), :]
         return remote(
             block, block, m_s.at[stream, index], m_r.at[stream, index], s, at.mate
         )
@@ -392,17 +448,12 @@
             index = 7 if step == 4 else 3 * way + step
             go(mate_copy(c, stream, index, k.came_from(way, step)))
 
-    def q_round(step):
-        for stream in (0, 1):
-            q.wait_z(stream, step - 1)
-            q.send_z(stream, step)
-
     def k_round(step):
-        for stream in (0, 1):
+        for stream in (0, 1, 2):
             k_arrived(stream, step - 1)
             k.send_z(stream, step)
 
-    q_round(2)
+    q.next_z(2)
     for m in range(4):
         @pl.when(4 * at.j + m != h)
         def _(m=m):
@@ -411,24 +462,20 @@
                 kv4.at[0], kvb.at[c, 0, rows, :], r_s.at[0], r_r.at[m], s, 4 * at.j + m
             ).wait_recv()
     k.start_y(k_source)
-    o.start_y(ow_source)
-    q_round(3)
-    k.wait_y(1, k_source)
-    k.send_z(0, 1)
-    go(mate_copy(c, 0, 0, at.z))
-    k.wait_y(2, k_source)
-    k.wait_y(3, k_source)
-    k.send_z(1, 1)
-    go(mate_copy(c, 1, 0, at.z))
+    o.start_half(ow)
+    for stream in (0, 1, 2):
+        if stream == 2:
+            q.next_z(3)
+        k.first_z(k_source, (stream,))
+        go(mate_copy(c, stream, 0, at.z))
     tok_copy.wait_recv()
     arrived_tokens = tokp.at[:, half_tokens]
     go(remote(arrived_tokens, arrived_tokens, e_s.at[13], e_r.at[13], s, at.mate))
-    q_round(4)
+    q.next_z(4)
     k_round(2)
     other_half = tokp.at[:, pl.ds(pl.multiple_of(1280 - 1280 * c, 128), 1280)]
     remote(other_half, other_half, e_s.at[13], e_r.at[13], s, at.mate).wait_recv()
-    q.wait_z(0, 4)
-    q.wait_z(1, 4)
+    q.end_z()
 
     def project_queries(source):
         total = jnp.zeros((128, 384), F32)
@@ -455,18 +502,17 @@
         )
     )
     k_round(3)
+    for i in (0, 1):
+        o.wait_half(i, ow)
+        o.send_z(i, 1)
     k_round(4)
-    o.wait_y(1, ow_source)
-    o.send_z(0, 1)
-    o.wait_y(2, ow_source)
-    o.wait_y(3, ow_source)
-    o.send_z(1, 1)
-    k_arrived(0, 4)
-    k_arrived(1, 4)
+    o.next_z(2)
+    for stream in (0, 1, 2):
+        k_arrived(stream, 4)
     q_in[0].wait_recv()
     q_in[2].wait_recv()
     q_in[1].wait_recv()
-    for stream in (0, 1):
+    for stream in (0, 1, 2):
         mate_copy(1 - c, stream, 0, at.z).wait_recv()
         for step in (1, 2, 3, 4):
             for way in k.ways(stream, step):
@@ -483,9 +529,7 @@
     attend_half(1, at, qbuf, stacked, kvb, scores, lane_max, store_part)
     part_copy = go(remote(part, part_in, e_s.at[4], e_r.at[4], s, at.head_pair))
     stat_copy = go(remote(stats, stats_in, e_s.at[5], e_r.at[5], s, at.head_pair))
-    for stream in (0, 1):
-        o.wait_z(stream, 1)
-        o.send_z(stream, 2)
+    o.next_z(3)
 
     def store_mine(head, row_max, row_total, numerator):
         mine[head] = numerator
@@ -493,9 +537,6 @@
         mine_total[head] = jnp.broadcast_to(row_total, (128, 128))
 
     attend_half(0, at, qbuf, stacked, kvb, scores, lane_max, store_mine)
-    for stream in (0, 1):
-        o.wait_z(stream, 2)
-        o.send_z(stream, 3)
     part_copy.wait_recv()
     stat_copy.wait_recv()
     for head in range(4):
@@ -508,53 +549,71 @@
         other_part = jnp.exp2((other_max - top) * EXP2_SCALE)
         total = mine_total[head] * own_part + other_total * other_part
         value = mine[head] * own_part + part_in[head].astype(F32) * other_part
-        attended[:, head * DV : (head + 1) * DV] = (value / total).astype(BF16)
-    for stream in (0, 1):
-        o.wait_z(stream, 3)
-        o.send_z(stream, 4)
-    o.wait_z(0, 4)
-    o.wait_z(1, 4)
-
-    for i in range(4):
-        start = pl.multiple_of(4 * ((at.y + i) % 4), 4)
+        attended[0:128, head * DV : (head + 1) * DV] = (value / total).astype(BF16)
+    attended_copy = go(
+        remote(
+            attended.at[0:128], attended.at[128:256], e_s.at[6], e_r.at[6], at.seq_pair, h
+        )
+    )
+    o.next_z(4)
+    o.end_z()
+    attended_copy.wait_recv()
+
+    for i in range(2):
         block = lax.dot_general(
             owb[i], attended[...], (((1,), (1,)), ((), ())), preferred_element_type=F32
-        ).reshape(2, 2, 160, 128)
-        summed[pl.ds(2 * ((at.y + i) % 4), 2)] = block
-        o1[pl.ds(2 * ((at.y + i) % 4), 2)] = block.astype(BF16)
-    mate_sum = go(remote(o1.at[:, 1 - c], o1_in, e_s.at[6], e_r.at[6], s, at.mate))
+        ).reshape(2, 2, 160, 256)
+        summed[2 * i : 2 * i + 2] = block
+        o1[2 * i : 2 * i + 2] = block.astype(BF16)
+    mate_sum = go(remote(o1.at[:, 1 - c], o1_in, e_s.at[14], e_r.at[14], s, at.mate))
     mate_sum.wait_recv()
-    for i in range(8):
-        summed[i, 0] = summed[i, c] + o1_in[i].astype(F32)
-        o2[i // 4, i % 4] = summed[i, 0].astype(BF16)
+    for x in range(4):
+        summed[x, 0] = summed[x, c] + o1_in[x].astype(F32)
+        o2[x] = summed[x, 0].astype(BF16)
     x_sums = []
     for d in (1, 2, 3):
         x = (at.x + d) % 4
         x_sums.append(
             go(
                 remote(
-                    o2.at[:, x], o2_in.at[d - 1], e_s.at[6 + d], e_r.at[6 + d], s, 8 * at.y_hi + 2 * x + c
+                    o2.at[x], o2_in.at[d - 1], e_s.at[6 + d], e_r.at[6 + d], s, 8 * at.y_hi + 2 * x + c
                 )
             )
         )
     for copy in x_sums:
         copy.wait_recv()
-    far = 1 - at.y_hi
-    value = summed[4 * far + at.x, 0]
+    value = summed[at.x, 0]
     for d in range(3):
-        value = value + o2_in[d, far].astype(F32)
-    o3[...] = value.astype(BF16)
-    y_sum = go(remote(o3, o3_in, e_s.at[10], e_r.at[10], s, at.head_far))
-    value = summed[4 * at.y_hi + at.x, 0]
-    for d in range(3):
-        value = value + o2_in[d, at.y_hi].astype(F32)
-    y_sum.wait_recv()
-    out[...] = (value + o3_in[...].astype(F32)).astype(BF16)
+        value = value + o2_in[d].astype(F32)
+    own, other = value[:, 0:128], value[:, 128:256]
+    o3[0] = own.astype(BF16)
+    o3[1] = other.astype(BF16)
+    own_sum = remote(o3.at[0], o3_in.at[1], e_s.at[10], e_r.at[10], s, at.head_far)
+    pair_sum = remote(o3.at[1], o3_in.at[0], e_s.at[15], e_r.at[15], at.seq_pair, h)
+    cross_sum = remote(o3.at[1], o3_in.at[1], e_s.at[10 + 6], e_r.at[10], at.seq_pair, at.head_far)
+
+    @pl.when(at.y_hi == at.parity)
+    def _():
+        pair_sum.start()
+        own_sum.wait_recv()
+        out[...] = (own + o3_in[1].astype(F32)).astype(BF16)
+        pair_sum.wait_send()
+
+    @pl.when(at.y_hi != at.parity)
+    def _():
+        cross_sum.start()
+        own_sum.start()
+        pair_sum.wait_recv()
+        cross_sum.wait_recv()
+        out[...] = (o3_in[0].astype(F32) + o3_in[1].astype(F32)).astype(BF16)
+        cross_sum.wait_send()
+        own_sum.wait_send()
 
     for copy in started:
         copy.wait_send()
     for gather in (q, k, o):
         gather.finish_sends()
+    o.end_half(ow)
     for group in range(G):
         @pl.when(4 * group + at.g != h)
         def _(group=group):
@@ -576,7 +635,7 @@
 ):
     vmem = pltpu.VMEM
     dma = pltpu.SemaphoreType.DMA
-    ring = [dma((4,)), dma((4,)), dma((2, 2, 4)), dma((2, 2, 4))]
+    ring = [dma((4,)), dma((4,)), dma((2, 3, 4)), dma((2, 3, 4))]
     out = pl.pallas_call(
         kernel,
         out_shape=jax.ShapeDtypeStruct((160, 128), BF16),
@@ -591,9 +650,8 @@
             vmem((272, 768), F32),
             vmem((64, 768), F32),
             vmem((G, 16, KV_WIDTH), BF16),
-            vmem((80, 512), BF16),
             vmem((4, 640, 384), BF16),
-            vmem((4, 640, 512), BF16),
+            vmem((2, 640, 512), BF16),
             vmem((2, 4, 512, KV_WIDTH), BF16),
             vmem((128, 2560), BF16),
             vmem((2, 2, 128, 384), BF16),
@@ -608,23 +666,23 @@
             vmem((4, 8, 128), F32),
             vmem((4, 128, 128), BF16),
             vmem((4, 8, 128), F32),
-            vmem((128, 512), BF16),
-            vmem((8, 2, 160, 128), F32),
-            vmem((8, 2, 160, 128), BF16),
-            vmem((8, 160, 128), BF16),
-            vmem((2, 4, 160, 128), BF16),
-            vmem((3, 2, 160, 128), BF16),
-            vmem((160, 128), BF16),
-            vmem((160, 128), BF16),
+            vmem((256, 512), BF16),
+            vmem((4, 2, 160, 256), F32),
+            vmem((4, 2, 160, 256), BF16),
+            vmem((4, 160, 256), BF16),
+            vmem((4, 160, 256), BF16),
+            vmem((3, 160, 256), BF16),
+            vmem((2, 160, 128), BF16),
+            vmem((2, 160, 128), BF16),
             *ring,
             *ring,
             *ring,
             dma((4,)),
             dma((4,)),
-            dma((2, 8)),
-            dma((2, 8)),
-            dma((14,)),
-            dma((14,)),
+            dma((3, 8)),
+            dma((3, 8)),
+            dma((17,)),
+            dma((17,)),
         ],
         compiler_params=pltpu.CompilerParams(
             collective_id=0, has_side_effects=True, vmem_limit_bytes=56 * 1024 * 1024
@@ -635,10 +693,10 @@
         raw_keys,
         raw_values,
         query_weight,
-        output_weight,
+        output_weight.T,
         key_expand,
         key_mix,
-        key_reduce,
+        key_reduce.T,
         value_expand,
         value_mix,
         value_reduce,

time: 111 us -> 100 us (0.901)
  Pallas kernels: 106 us -> 98.4 us
  local copies, waits for them, and re-layouts: 4.91 us -> 1.4 us
    pallas_call x1, Pallas kernels: 106 us -> 98.4 us  [shards(): pl.pallas_call(kernel, out_shape=jax.ShapeDtypeStruct((160, 128), BF16),...]
    unnamed x3 -> x1, local copies, waits for them, and re-layouts: 4.91 us -> 1.4 us
where the time goes in v3:
time: 100 us; the launch traced here: 99.8 us
  Pallas kernels  98.4 us (98%)
  local copies, waits for them, and re-layouts  1.4 us (1%)
    pallas_call x1, Pallas kernels, shards(): pl.pallas_call(kernel, out_shape=jax.ShapeDtypeStruct((160, 128), BF16),...  98.4 us

profile of v3, /device:TPU:1, one launch (start us, length us, event | category | flops | bytes accessed | tf_op | source)
XLA Modules:
  0.0 99.8 jit_solution(14017491783905357236)
XLA Ops:
  0.0 98.4 %branch.1 = bf16[160,128]{1,0:T(8,128)(2,1)} custom-call(bf16[128,2560]{1,0:T(8,128)(2,1)} %tokens.1, bf16[256,768]{1,0:T(8,128)(2,1)} %raw_keys.1, bf16[256,512]{1,0:T(8,128)(2,1)} %raw_values.1, bf16[80,768]{1,0:T(8,128)(2,1)} %qw.1, bf16[80,512]{1,0:T(8,128)(2,1)} %bitcast.5, bf16[192,768]{1,0:T(8,128)(2,1)} %key_expand.1, f32[32,768]{1,0:T(8,128)} %key_mix.1, ...), custom_call_target="tpu_custom_call" | custom-call | tf_op jit(solution)/shard_map/branch/pallas_call | solution.py:639
  98.4 1.4 %copy.13 = bf16[128,160]{0,1:T(8,128)(2,1)} copy(bf16[128,160]{0,1:T(8,128)(2,1)} %bitcast.4) | data formatting | bytes 81920

commit v4 on v3

--- a/solution.py
+++ b/solution.py
@@ -313,6 +313,7 @@
     r_s, r_r,
     m_s, m_r,
     e_s, e_r,
+    t_s, t_r,
 ):
     at = Place()
     s, h, c = at.s, at.h, at.core
@@ -355,12 +356,6 @@
     ]
     q.start_y(q_source)
     q.first_z(q_source, (0,))
-    half_tokens = pl.ds(pl.multiple_of(1280 * c, 128), 1280)
-    tok_copy = go(
-        remote(
-            tokens.at[:, half_tokens], tokp.at[:, half_tokens], e_s.at[0], e_r.at[0], at.seq_pair, h
-        )
-    )
     placed_expand[0, 0:DK, :] = key_expand[...]
     placed_expand[0, DK:256, :] = jnp.zeros((256 - DK, 768), BF16)
     placed_expand[1, 0 : 256 - DK, :] = jnp.zeros((256 - DK, 768), BF16)
@@ -462,20 +457,27 @@
                 kv4.at[0], kvb.at[c, 0, rows, :], r_s.at[0], r_r.at[m], s, 4 * at.j + m
             ).wait_recv()
     k.start_y(k_source)
+    half_tokens = pl.ds(pl.multiple_of(1280 * c, 128), 1280)
+    tok_copy = go(
+        remote(
+            tokens.at[:, half_tokens], tokp.at[:, half_tokens], e_s.at[0], e_r.at[0], at.seq_pair, h
+        )
+    )
     o.start_half(ow)
-    for stream in (0, 1, 2):
-        if stream == 2:
-            q.next_z(3)
+    k.first_z(k_source, (0,))
+    go(mate_copy(c, 0, 0, at.z))
+    q.next_z(3)
+    for stream in (1, 2):
         k.first_z(k_source, (stream,))
         go(mate_copy(c, stream, 0, at.z))
+    q.next_z(4)
+    k_round(2)
     tok_copy.wait_recv()
     arrived_tokens = tokp.at[:, half_tokens]
     go(remote(arrived_tokens, arrived_tokens, e_s.at[13], e_r.at[13], s, at.mate))
-    q.next_z(4)
-    k_round(2)
+    q.end_z()
     other_half = tokp.at[:, pl.ds(pl.multiple_of(1280 - 1280 * c, 128), 1280)]
     remote(other_half, other_half, e_s.at[13], e_r.at[13], s, at.mate).wait_recv()
-    q.end_z()
 
     def project_queries(source):
         total = jnp.zeros((128, 384), F32)
@@ -557,52 +559,67 @@
     )
     o.next_z(4)
     o.end_z()
-    attended_copy.wait_recv()
-
-    for i in range(2):
-        block = lax.dot_general(
-            owb[i], attended[...], (((1,), (1,)), ((), ())), preferred_element_type=F32
-        ).reshape(2, 2, 160, 256)
-        summed[2 * i : 2 * i + 2] = block
-        o1[2 * i : 2 * i + 2] = block.astype(BF16)
-    mate_sum = go(remote(o1.at[:, 1 - c], o1_in, e_s.at[14], e_r.at[14], s, at.mate))
-    mate_sum.wait_recv()
-    for x in range(4):
-        summed[x, 0] = summed[x, c] + o1_in[x].astype(F32)
-        o2[x] = summed[x, 0].astype(BF16)
-    x_sums = []
-    for d in (1, 2, 3):
-        x = (at.x + d) % 4
-        x_sums.append(
-            go(
-                remote(
-                    o2.at[x], o2_in.at[d - 1], e_s.at[6 + d], e_r.at[6 + d], s, 8 * at.y_hi + 2 * x + c
-                )
+
+    mate_sums = []
+    for n in range(2):
+        if n == 1:
+            attended_copy.wait_recv()
+        for i in range(2):
+            block = lax.dot_general(
+                owb[i],
+                attended[128 * n : 128 * (n + 1)],
+                (((1,), (1,)), ((), ())),
+                preferred_element_type=F32,
+            ).reshape(2, 2, 160, 128)
+            summed[n, 2 * i : 2 * i + 2] = block
+            o1[n, 2 * i : 2 * i + 2] = block.astype(BF16)
+        mate_sums.append(
+            go(remote(o1.at[n, :, 1 - c], o1_in.at[n], t_s.at[n, 0], t_r.at[n, 0], s, at.mate))
+        )
+    x_sums = [[], []]
+    for n in range(2):
+        mate_sums[n].wait_recv()
+        for x in range(4):
+            summed[n, x, 0] = summed[n, x, c] + o1_in[n, x].astype(F32)
+            o2[n, x] = summed[n, x, 0].astype(BF16)
+        for d in (1, 2, 3):
+            x = (at.x + d) % 4
+            target = 8 * at.y_hi + 2 * x + c
+            x_sums[n].append(
+                go(remote(o2.at[n, x], o2_in.at[n, d - 1], t_s.at[n, d], t_r.at[n, d], s, target))
             )
-        )
-    for copy in x_sums:
-        copy.wait_recv()
-    value = summed[at.x, 0]
-    for d in range(3):
-        value = value + o2_in[d].astype(F32)
-    own, other = value[:, 0:128], value[:, 128:256]
+
+    def x_total(n):
+        for copy in x_sums[n]:
+            copy.wait_recv()
+        value = summed[n, at.x, 0]
+        for d in range(3):
+            value = value + o2_in[n, d].astype(F32)
+        return value
+
+    final_here = at.y_hi == at.parity
+    own_sum = remote(o3.at[0], o3_in.at[1], t_s.at[0, 4], t_r.at[0, 4], s, at.head_far)
+    cross_sum = remote(o3.at[1], o3_in.at[1], t_s.at[1, 4], t_r.at[0, 4], at.seq_pair, at.head_far)
+    pair_sum = remote(o3.at[1], o3_in.at[0], t_s.at[1, 4], t_r.at[1, 4], at.seq_pair, h)
+    own = x_total(0)
     o3[0] = own.astype(BF16)
-    o3[1] = other.astype(BF16)
-    own_sum = remote(o3.at[0], o3_in.at[1], e_s.at[10], e_r.at[10], s, at.head_far)
-    pair_sum = remote(o3.at[1], o3_in.at[0], e_s.at[15], e_r.at[15], at.seq_pair, h)
-    cross_sum = remote(o3.at[1], o3_in.at[1], e_s.at[10 + 6], e_r.at[10], at.seq_pair, at.head_far)
-
-    @pl.when(at.y_hi == at.parity)
+
+    @pl.when(jnp.logical_not(final_here))
+    def _():
+        own_sum.start()
+
+    o3[1] = x_total(1).astype(BF16)
+
+    @pl.when(final_here)
     def _():
         pair_sum.start()
         own_sum.wait_recv()
         out[...] = (own + o3_in[1].astype(F32)).astype(BF16)
         pair_sum.wait_send()
 
-    @pl.when(at.y_hi != at.parity)
+    @pl.when(jnp.logical_not(final_here))
     def _():
         cross_sum.start()
-        own_sum.start()
         pair_sum.wait_recv()
         cross_sum.wait_recv()
         out[...] = (o3_in[0].astype(F32) + o3_in[1].astype(F32)).astype(BF16)
@@ -667,11 +684,11 @@
             vmem((4, 128, 128), BF16),
             vmem((4, 8, 128), F32),
             vmem((256, 512), BF16),
-            vmem((4, 2, 160, 256), F32),
-            vmem((4, 2, 160, 256), BF16),
-            vmem((4, 160, 256), BF16),
-            vmem((4, 160, 256), BF16),
-            vmem((3, 160, 256), BF16),
+            vmem((2, 4, 2, 160, 128), F32),
+            vmem((2, 4, 2, 160, 128), BF16),
+            vmem((2, 4, 160, 128), BF16),
+            vmem((2, 4, 160, 128), BF16),
+            vmem((2, 3, 160, 128), BF16),
             vmem((2, 160, 128), BF16),
             vmem((2, 160, 128), BF16),
             *ring,
@@ -681,8 +698,10 @@
             dma((4,)),
             dma((3, 8)),
             dma((3, 8)),
-            dma((17,)),
-            dma((17,)),
+            dma((14,)),
+            dma((14,)),
+            dma((2, 5)),
+            dma((2, 5)),
         ],
         compiler_params=pltpu.CompilerParams(
             collective_id=0, has_side_effects=True, vmem_limit_bytes=56 * 1024 * 1024

time: 100 us -> 94.3 us (0.943); the launches traced: 99.8 us -> 92.9 us
  Pallas kernels: 98.4 us -> 91.5 us
    pallas_call x1, Pallas kernels: 98.4 us -> 91.5 us  [shards(): pl.pallas_call(kernel, out_shape=jax.ShapeDtypeStruct((160, 128), BF16),...]
where the time goes in v4:
time: 94.3 us; the launch traced here: 92.9 us
  Pallas kernels  91.5 us (97%)
  local copies, waits for them, and re-layouts  1.4 us (1%)
    pallas_call x1, Pallas kernels, shards(): pl.pallas_call(kernel, out_shape=jax.ShapeDtypeStruct((160, 128), BF16),...  91.5 us

profile of v4, /device:TPU:1, one launch (start us, length us, event | category | flops | bytes accessed | tf_op | source)
XLA Modules:
  0.0 92.9 jit_solution(12037166947827730124)
XLA Ops:
  0.0 91.5 %branch.1 = bf16[160,128]{1,0:T(8,128)(2,1)} custom-call(bf16[128,2560]{1,0:T(8,128)(2,1)} %tokens.1, bf16[256,768]{1,0:T(8,128)(2,1)} %raw_keys.1, bf16[256,512]{1,0:T(8,128)(2,1)} %raw_values.1, bf16[80,768]{1,0:T(8,128)(2,1)} %qw.1, bf16[80,512]{1,0:T(8,128)(2,1)} %bitcast.5, bf16[192,768]{1,0:T(8,128)(2,1)} %key_expand.1, f32[32,768]{1,0:T(8,128)} %key_mix.1, ...), custom_call_target="tpu_custom_call" | custom-call | tf_op jit(solution)/shard_map/branch/pallas_call | solution.py:656
  91.5 1.4 %copy.13 = bf16[128,160]{0,1:T(8,128)(2,1)} copy(bf16[128,160]{0,1:T(8,128)(2,1)} %bitcast.4) | data formatting | bytes 81920

commit v5 on v4

--- a/solution.py
+++ b/solution.py
@@ -11,7 +11,6 @@
 CTX = 126976
 DK = 192
 DV = 128
-KV_WIDTH = 384
 SEQ_HEAD = ("seq", "head")
 MESH = pl.DeviceIdType.MESH
 BF16 = jnp.bfloat16
@@ -206,59 +205,70 @@
 HALVES = ((0, 1, 0), (1, 1, 1))
 
 
-def attend_half(who, at, qbuf, stacked, kvb, scores, lane_max, store):
+def attend_half(who, at, qbuf, stacked, kvb, scores, lane_max, store, hooks):
     for half in range(2):
         for head in range(2):
             rows = pl.ds((2 * half + head) * 128, 128)
-            stacked[rows, 0:DK] = qbuf[who, half, :, head * DK : (head + 1) * DK]
+            queries = qbuf[who, half, :, head * DK : (head + 1) * DK]
+            stacked[0, rows, 0:DK] = queries
+            stacked[1, rows, 0:128] = queries[:, 0:128]
+            stacked[1, rows, DK:256] = queries[:, 128:DK]
     last = (3 + 4 - at.y) % 4
     first_position = CTX + at.s * 128
     half_index = (at.h // 2) % 2
 
     def entry(n):
-        return n // 4, (last + n % 4) % 4
+        return (at.core + n // 4) % 2, (last + n % 4) % 4
+
+    def rows_of(n, start):
+        quarter, i = entry(n)
+        return kvb[quarter, i].reshape(8, 160, 128)[:, start : start + 32].reshape(256, 128)
 
     def score_chunk(n, masked):
-        quarter, i = entry(n)
-        block = lax.dot_general(
-            stacked[...], kvb[quarter, i, :, 0:256], (((1,), (1,)), ((), ())), preferred_element_type=F32
-        )
-        parts = [block[:, 128 * k : 128 * (k + 1)] for k in range(4)]
-        if masked:
-            column = lax.broadcasted_iota(jnp.int32, (512, 128), 1)
-            row = lax.broadcasted_iota(jnp.int32, (512, 128), 0) % 128
-            ids = 256 * (30 + column // 64) + 64 * (2 * half_index + quarter) + column % 64
-            visible = STRIDE * ids + BLK - 1 <= first_position + row
-            parts[3] = jnp.where(visible, parts[3], -jnp.inf)
+        quarter, _ = entry(n)
+        upper = rows_of(n, 128)
+        parts = []
+        for side in range(2):
+            keys = jnp.concatenate([rows_of(n, 32 * side), upper], axis=1)
+            block = lax.dot_general(
+                stacked[side], keys, (((1,), (1,)), ((), ())), preferred_element_type=F32
+            )
+            parts.append(block[:, 0:128])
+            tail = block[:, 128:256]
+            if masked:
+                column = lax.broadcasted_iota(jnp.int32, (512, 128), 1)
+                row = lax.broadcasted_iota(jnp.int32, (512, 128), 0) % 128
+                ids = 256 * (28 + column // 32) + 64 * (2 * half_index + quarter)
+                ids = ids + 32 * side + column % 32
+                visible = STRIDE * ids + BLK - 1 <= first_position + row
+                tail = jnp.where(visible, tail, -jnp.inf)
+            parts.append(tail)
         for k in range(4):
             scores[n, :, 128 * k : 128 * (k + 1)] = parts[k]
         return jnp.maximum(jnp.maximum(parts[0], parts[1]), jnp.maximum(parts[2], parts[3]))
 
-    lane_max[...] = jnp.maximum(score_chunk(0, True), score_chunk(4, True))
-
-    def other_chunk(n, carry):
-        lane_max[...] = jnp.maximum(lane_max[...], score_chunk(n + n // 3 + 1, False))
-        return carry
-
-    lax.fori_loop(0, 6, other_chunk, 0, unroll=6)
+    lane_max[...] = score_chunk(0, True)
+    for n in (1, 2, 3):
+        lane_max[...] = jnp.maximum(lane_max[...], score_chunk(n, False))
+    hooks[0]()
+    lane_max[...] = jnp.maximum(lane_max[...], score_chunk(4, True))
+    for n in (5, 6, 7):
+        lane_max[...] = jnp.maximum(lane_max[...], score_chunk(n, False))
+    hooks[1]()
 
     for head in range(4):
         rows = slice(head * 128, (head + 1) * 128)
         row_max = jnp.max(lane_max[rows, :], axis=1, keepdims=True)
-
-        def weigh_chunk(n, carry):
-            total, numerator = carry
+        total = jnp.zeros((128, 128), F32)
+        numerator = jnp.zeros((128, 128), F32)
+        for n in range(8):
             exponent = jnp.exp2((scores[n, rows, :] - row_max) * EXP2_SCALE)
             for k in range(4):
                 total = total + exponent[:, 128 * k : 128 * (k + 1)]
-            quarter, i = entry(n)
+            values = jnp.concatenate([rows_of(n, 64), rows_of(n, 96)], axis=0)
             numerator = numerator + jnp.dot(
-                exponent.astype(BF16), kvb[quarter, i, :, 256:384], preferred_element_type=F32
+                exponent.astype(BF16), values, preferred_element_type=F32
             )
-            return total, numerator
-
-        start = jnp.zeros((128, 128), F32)
-        total, numerator = lax.fori_loop(0, 8, weigh_chunk, (start, start), unroll=8)
         store(head, row_max, jnp.sum(total, axis=1, keepdims=True), numerator)
 
 
@@ -283,6 +293,7 @@
     projected,
     hidden,
     kv4,
+    kvt,
     qwb,
     owb,
     kvb,
@@ -339,7 +350,7 @@
 
     q = Gather(at, qwb, 80, QUARTERS, (q_ys, q_yr, q_zs, q_zr))
     o = HalfGather(at, owb, 80, HALVES, (o_ys, o_yr, o_zs, o_zr))
-    k = Gather(at, kvb.at[c], 64, QUARTERS, (k_ys, k_yr, k_zs, k_zr))
+    k = Gather(at, kvb.at[c], 160, QUARTERS, (k_ys, k_yr, k_zs, k_zr))
 
     edge_in = [
         remote(source.at[0:16], target, e_s.at[i], e_r.at[i], before // 16, before % 16)
@@ -360,7 +371,8 @@
     placed_expand[0, DK:256, :] = jnp.zeros((256 - DK, 768), BF16)
     placed_expand[1, 0 : 256 - DK, :] = jnp.zeros((256 - DK, 768), BF16)
     placed_expand[1, 256 - DK :, :] = key_expand[...]
-    stacked[:, DK:] = jnp.zeros((512, 256 - DK), BF16)
+    stacked[0, :, DK:] = jnp.zeros((512, 256 - DK), BF16)
+    stacked[1, :, 128:DK] = jnp.zeros((512, DK - 128), BF16)
 
     q.first_z(q_source, (1, 2))
 
@@ -400,22 +412,13 @@
     )
     for group in range(G):
         rows = slice(16 * group, 16 * group + 16)
-        kv4[group, :, 0:DK] = packed_keys[rows, :]
-        kv4[group, :, DK:256] = jnp.zeros((16, 256 - DK), BF16)
-        kv4[group, :, 256:384] = packed_values[rows, :]
-
-    own_rows = pl.ds(pl.multiple_of(64 * at.z + 16 * at.j, 16), 16)
+        kv4[group, 0:16, :] = packed_keys[rows, 0:128]
+        kv4[group, 16:32, :] = packed_values[rows, :]
+        kv4[group, 32:48, 0:64] = packed_keys[rows, 128:DK]
+        kv4[group, 32:48, 64:128] = packed_keys[rows, 128:DK]
 
     def spread_copy(group):
-        quarter = at.g % 2
-        return remote(
-            kv4.at[group],
-            kvb.at[quarter, 0, own_rows, :],
-            r_s.at[group],
-            r_r.at[at.j],
-            s,
-            4 * group + at.g,
-        )
+        return remote(kv4.at[group], kvt.at[at.j], r_s.at[group], r_r.at[at.j], s, 4 * group + at.g)
 
     for group in range(G):
         @pl.when(4 * group + at.g != h)
@@ -424,15 +427,15 @@
 
         @pl.when(4 * group + at.g == h)
         def _(group=group):
-            kvb[c, 0, own_rows, :] = kv4[group]
+            kvt[at.j] = kv4[group]
 
     def k_source(target):
         return k.piece(0, at.z)
 
     def mate_copy(quarter, stream, index, z):
         first, count, _ = QUARTERS[stream]
-        start = pl.multiple_of(64 * z, 16)
-        block = kvb.at[quarter, pl.ds(first, count), pl.ds(start, 64), :]
+        start = pl.multiple_of(160 * z, 16)
+        block = kvb.at[quarter, pl.ds(first, count), pl.ds(start, 160), :]
         return remote(
             block, block, m_s.at[stream, index], m_r.at[stream, index], s, at.mate
         )
@@ -452,10 +455,19 @@
     for m in range(4):
         @pl.when(4 * at.j + m != h)
         def _(m=m):
-            rows = pl.ds(pl.multiple_of(64 * at.z + 16 * m, 16), 16)
             remote(
-                kv4.at[0], kvb.at[c, 0, rows, :], r_s.at[0], r_r.at[m], s, 4 * at.j + m
+                kv4.at[0], kvt.at[m], r_s.at[0], r_r.at[m], s, 4 * at.j + m
             ).wait_recv()
+    piece = pl.multiple_of(160 * at.z, 16)
+    left_lanes = lax.broadcasted_iota(jnp.int32, (16, 128), 1) < 64
+    for m in range(4):
+        kvb[c, 0, pl.ds(piece + 16 * m, 16), :] = kvt[m, 0:16, :]
+        kvb[c, 0, pl.ds(piece + 64 + 16 * m, 16), :] = kvt[m, 16:32, :]
+    for m in range(2):
+        both = jnp.where(
+            left_lanes, kvt[m, 32:48, :].astype(F32), kvt[m + 2, 32:48, :].astype(F32)
+        )
+        kvb[c, 0, pl.ds(piece + 128 + 16 * m, 16), :] = both.astype(BF16)
     k.start_y(k_source)
     half_tokens = pl.ds(pl.multiple_of(1280 * c, 128), 1280)
     tok_copy = go(
@@ -514,12 +526,16 @@
     q_in[0].wait_recv()
     q_in[2].wait_recv()
     q_in[1].wait_recv()
-    for stream in (0, 1, 2):
-        mate_copy(1 - c, stream, 0, at.z).wait_recv()
-        for step in (1, 2, 3, 4):
-            for way in k.ways(stream, step):
-                index = 7 if step == 4 else 3 * way + step
-                mate_copy(1 - c, stream, index, k.came_from(way, step)).wait_recv()
+    def mate_arrived():
+        for stream in (0, 1, 2):
+            mate_copy(1 - c, stream, 0, at.z).wait_recv()
+            for step in (1, 2, 3, 4):
+                for way in k.ways(stream, step):
+                    index = 7 if step == 4 else 3 * way + step
+                    mate_copy(1 - c, stream, index, k.came_from(way, step)).wait_recv()
+
+    def nothing():
+        pass
 
     lane = lax.broadcasted_iota(jnp.int32, (128, 128), 1)
 
@@ -528,17 +544,16 @@
         tile = jnp.where(lane == 0, row_max, jnp.where(lane == 1, row_total, 0.0))
         stats[head] = jnp.transpose(tile)[0:8, :]
 
-    attend_half(1, at, qbuf, stacked, kvb, scores, lane_max, store_part)
+    attend_half(1, at, qbuf, stacked, kvb, scores, lane_max, store_part, (mate_arrived, lambda: o.next_z(3)))
     part_copy = go(remote(part, part_in, e_s.at[4], e_r.at[4], s, at.head_pair))
     stat_copy = go(remote(stats, stats_in, e_s.at[5], e_r.at[5], s, at.head_pair))
-    o.next_z(3)
 
     def store_mine(head, row_max, row_total, numerator):
         mine[head] = numerator
         mine_max[head] = jnp.broadcast_to(row_max, (128, 128))
         mine_total[head] = jnp.broadcast_to(row_total, (128, 128))
 
-    attend_half(0, at, qbuf, stacked, kvb, scores, lane_max, store_mine)
+    attend_half(0, at, qbuf, stacked, kvb, scores, lane_max, store_mine, (nothing, lambda: o.next_z(4)))
     part_copy.wait_recv()
     stat_copy.wait_recv()
     for head in range(4):
@@ -557,7 +572,6 @@
             attended.at[0:128], attended.at[128:256], e_s.at[6], e_r.at[6], at.seq_pair, h
         )
     )
-    o.next_z(4)
     o.end_z()
 
     mate_sums = []
@@ -666,14 +680,15 @@
             vmem((2, 256, 768), BF16),
             vmem((272, 768), F32),
             vmem((64, 768), F32),
-            vmem((G, 16, KV_WIDTH), BF16),
+            vmem((G, 48, 128), BF16),
+            vmem((4, 48, 128), BF16),
             vmem((4, 640, 384), BF16),
             vmem((2, 640, 512), BF16),
-            vmem((2, 4, 512, KV_WIDTH), BF16),
+            vmem((2, 4, 1280, 128), BF16),
             vmem((128, 2560), BF16),
             vmem((2, 2, 128, 384), BF16),
             vmem((128, 384), BF16),
-            vmem((512, 256), BF16),
+            vmem((2, 512, 256), BF16),
             vmem((8, 512, 512), F32),
             vmem((512, 128), F32),
             vmem((4, 128, 128), F32),

time: 94.3 us -> 90.9 us (0.964)
  the two profiles are of different devices: /device:TPU:1 before, /device:TPU:8 now
where the time goes in v5:
time: 90.9 us; the launch traced here: 90.7 us
  Pallas kernels  89.3 us (98%)
  local copies, waits for them, and re-layouts  1.4 us (2%)
    pallas_call x1, Pallas kernels, shards(): pl.pallas_call(kernel, out_shape=jax.ShapeDtypeStruct((160, 128), BF16),...  89.3 us

profile of v5, /device:TPU:8, one launch (start us, length us, event | category | flops | bytes accessed | tf_op | source)
XLA Modules:
  0.0 90.7 jit_solution(11843016656983385373)
XLA Ops:
  0.0 89.3 %branch.1 = bf16[160,128]{1,0:T(8,128)(2,1)} custom-call(bf16[128,2560]{1,0:T(8,128)(2,1)} %tokens.1, bf16[256,768]{1,0:T(8,128)(2,1)} %raw_keys.1, bf16[256,512]{1,0:T(8,128)(2,1)} %raw_values.1, bf16[80,768]{1,0:T(8,128)(2,1)} %qw.1, bf16[80,512]{1,0:T(8,128)(2,1)} %bitcast.5, bf16[192,768]{1,0:T(8,128)(2,1)} %key_expand.1, f32[32,768]{1,0:T(8,128)} %key_mix.1, ...), custom_call_target="tpu_custom_call" | custom-call | tf_op jit(solution)/shard_map/branch/pallas_call | solution.py:670
  89.3 1.4 %copy.13 = bf16[128,160]{0,1:T(8,128)(2,1)} copy(bf16[128,160]{0,1:T(8,128)(2,1)} %bitcast.4) | data formatting | bytes 81920
